TPU v7x, 32 devices: a whole 2x2x4 slice. The times are simulated.
32 devices in a mesh: rep: 2 (over x), tp: 4 (over z), sp: 4 (over y, core).
Axes of the slice: x: 2, y: 2, z: 4, core: 2. Of those that a mesh axis runs over, the one named last changes fastest.
Arguments:
- x_in: bfloat16 [8192, 5120], P(('rep', 'sp')), parts along dimension 0
- positions: int32 [8192], P(('rep', 'sp')), parts along dimension 0
- norm_gain: float32 [5120], replicated
- w_q: bfloat16 [5120, 4096], P(None, 'tp')
- w_k: bfloat16 [5120, 1024], P(None, 'tp')
- w_v: bfloat16 [5120, 1024], P(None, 'tp')
- w_o: bfloat16 [4096, 5120], P('tp')
- w_gate: bfloat16 [5120, 32768], P(None, 'tp')
- w_up: bfloat16 [5120, 32768], P(None, 'tp')
- w_down: bfloat16 [32768, 5120], P('tp')
Outputs:
- output 1: bfloat16 [8192, 5120], P(('rep', 'sp')), parts along dimension 0
- output 2: bfloat16 [8192, 16, 128], P('rep', ('tp', 'sp')), parts along dimension 0
- output 3: bfloat16 [8192, 16, 128], P('rep', ('tp', 'sp')), parts along dimension 0
There are 2 independent parts. A program takes and returns all parts, laid end to end along the dimension named above; an argument that names none is the same for every part.
All inputs are finite; a program needn't handle non-finite values.
Results may differ from a plain program's by a relative error of at most 0.00245318.
Values are sent between devices in bfloat16 or wider.
A program may use at most 1.25 GiB of HBM per device.

v0:
```python
import jax
import jax.numpy as jnp
from jax import lax
from jax.sharding import PartitionSpec as P

HEAD_DIM = 128
EPS = 1e-6
ROPE_BASE = 500000.0
SCORE_SCALE = HEAD_DIM ** -0.5


def rms_norm(x_in, norm_gain):
    x_f32 = x_in.astype(jnp.float32)
    inv_rms = lax.rsqrt(jnp.mean(x_f32 * x_f32, axis=-1, keepdims=True) + EPS)
    return (x_f32 * inv_rms * norm_gain).astype(jnp.bfloat16)


def rope_tables(positions):
    inv_freq = ROPE_BASE ** (-(jnp.arange(HEAD_DIM // 2, dtype=jnp.float32) * (2.0 / HEAD_DIM)))
    angles = positions.astype(jnp.float32)[:, None] * inv_freq[None, :]
    return jnp.cos(angles)[:, None, :], jnp.sin(angles)[:, None, :]


def rotate(vectors, cos_tab, sin_tab):
    half_dim = HEAD_DIM // 2
    lower_part = vectors[..., :half_dim]
    upper_part = vectors[..., half_dim:]
    return jnp.concatenate([lower_part * cos_tab - upper_part * sin_tab, upper_part * cos_tab + lower_part * sin_tab], axis=-1).astype(jnp.bfloat16)


def gated_mlp(normed, w_gate, w_up, w_down):
    gate_acc = jnp.dot(normed, w_gate, preferred_element_type=jnp.float32)
    up_acc = jnp.dot(normed, w_up, preferred_element_type=jnp.float32)
    hidden = (jax.nn.silu(gate_acc) * up_acc).astype(jnp.bfloat16)
    return jnp.dot(hidden, w_down, preferred_element_type=jnp.float32)


def causal_attention(q_rows, k_keys, v_keys, q_offset):
    tokens_q = q_rows.shape[0]
    heads_here = q_rows.shape[1]
    key_count = k_keys.shape[0]
    cache_here = k_keys.shape[1]
    group_size = heads_here // cache_here
    tile_rows = min(tokens_q, 128)
    key_idx = jnp.arange(key_count)

    def attend_tile(tile_id):
        q_tile = lax.dynamic_slice_in_dim(q_rows, tile_id * tile_rows, tile_rows, axis=0).reshape(tile_rows, cache_here, group_size, HEAD_DIM)
        scores = jnp.einsum("qcgd,kcd->cgqk", q_tile, k_keys, preferred_element_type=jnp.float32) * SCORE_SCALE
        query_idx = q_offset + tile_id * tile_rows + jnp.arange(tile_rows)
        scores = jnp.where(key_idx[None, :] <= query_idx[:, None], scores, -jnp.inf)
        weights = jnp.exp(scores - jnp.max(scores, axis=-1, keepdims=True))
        weight_total = jnp.sum(weights, axis=-1)
        weighted_sum = jnp.einsum("cgqk,kcd->qcgd", weights.astype(jnp.bfloat16), v_keys, preferred_element_type=jnp.float32)
        return (weighted_sum / jnp.transpose(weight_total, (2, 0, 1))[..., None]).astype(jnp.bfloat16)

    attn_tiles = lax.map(attend_tile, jnp.arange(tokens_q // tile_rows))
    return attn_tiles.reshape(tokens_q, heads_here, HEAD_DIM)


def solution(mesh):
    sp_size = mesh.shape["sp"]
    row_spec = P(("rep", "sp"), None)
    cache_spec = P("rep", ("tp", "sp"), None)

    def layer_block(x_in, positions, norm_gain, w_q, w_k, w_v, w_o, w_gate, w_up, w_down):
        tok_local = x_in.shape[0]
        heads_tp = w_q.shape[1] // HEAD_DIM
        kv_tp = w_k.shape[1] // HEAD_DIM
        heads_dev = heads_tp // sp_size
        cache_tp = max(kv_tp, sp_size)
        cache_dev = cache_tp // sp_size
        kv_repeat = cache_tp // kv_tp
        normed = rms_norm(x_in, norm_gain)
        cos_tab, sin_tab = rope_tables(positions)
        q_rot = rotate(jnp.dot(normed, w_q, preferred_element_type=jnp.float32).reshape(tok_local, heads_tp, HEAD_DIM), cos_tab, sin_tab)
        k_rot = rotate(jnp.dot(normed, w_k, preferred_element_type=jnp.float32).reshape(tok_local, kv_tp, HEAD_DIM), cos_tab, sin_tab)
        v_val = jnp.dot(normed, w_v, preferred_element_type=jnp.float32).astype(jnp.bfloat16).reshape(tok_local, kv_tp, HEAD_DIM)
        q_send = q_rot.reshape(tok_local, sp_size, heads_dev, HEAD_DIM)
        k_send = jnp.repeat(k_rot, kv_repeat, axis=1).reshape(tok_local, sp_size, cache_dev, HEAD_DIM)
        v_send = jnp.repeat(v_val, kv_repeat, axis=1).reshape(tok_local, sp_size, cache_dev, HEAD_DIM)
        send_buf = jnp.concatenate([q_send, k_send, v_send], axis=2)
        recv_buf = lax.all_to_all(send_buf, "sp", 1, 0, tiled=True)
        recv_buf = recv_buf.reshape(tok_local * sp_size, heads_dev + 2 * cache_dev, HEAD_DIM)
        q_all = recv_buf[:, :heads_dev]
        k_all = recv_buf[:, heads_dev:heads_dev + cache_dev]
        v_all = recv_buf[:, heads_dev + cache_dev:]
        attn_heads = causal_attention(q_all, k_all, v_all, 0)
        attn_tok = lax.all_to_all(attn_heads, "sp", 0, 1, tiled=True).reshape(tok_local, heads_tp * HEAD_DIM)
        attn_sum = lax.psum(jnp.dot(attn_tok, w_o, preferred_element_type=jnp.float32), "tp")
        mlp_sum = lax.psum(gated_mlp(normed, w_gate, w_up, w_down), "tp")
        y_out = (x_in.astype(jnp.float32) + attn_sum + mlp_sum).astype(jnp.bfloat16)
        return y_out, k_all, v_all

    return jax.shard_map(
        layer_block,
        mesh=mesh,
        in_specs=(row_spec, P(("rep", "sp")), P(None), P(None, "tp"), P(None, "tp"), P(None, "tp"), P("tp", None), P(None, "tp"), P(None, "tp"), P("tp", None)),
        out_specs=(row_spec, cache_spec, cache_spec),
        check_vma=False,
    )
```

profile of v0, /device:TPU:5, one launch (start us, length us, event | category | flops | bytes accessed | tf_op | source)
XLA Modules:
  0.0 1981.7 jit_solution(12450708576878503818)
XLA Ops:
  8.1 6.5 fusion.29
  15.0 3.3 convolution_convert_fusion
  18.5 7.8 fusion.38
  27.8 18.6 fusion.40
  46.4 4.3 subtract_convert_fusion
  50.6 2.0 copy.29
  52.7 2.8 copy.30
  55.7 3.9 pad_maximum_fusion
  59.6 5.1 all-to-all-start
  64.6 97.1 %fusion.35 = f32[1024,8192]{1,0:T(8,128)} fusion(bf16[5120,8192]{1,0:T(8,128)(2,1)} %param.19, bf16[1024,5120]{1,0:T(8,128)(2,1)} %param.12, f32[5120]{0:T(1024)S(1)} %copy-done.5, f32[1024]{0:T(1024)S(1)} %add_rsqrt_fusion), kind=kOutput, calls=%fused_computation.41 | convolution fusion | flops 85920317440 | bytes 127950848 | tf_op jit(solution)/shard_map/dot_general | solution.py:32
  161.8 100.4 %multiply_convert_fusion = bf16[1024,8192]{1,0:T(8,128)(2,1)} fusion(f32[1024,8192]{1,0:T(8,128)} %fusion.35, bf16[5120,8192]{1,0:T(8,128)(2,1)} %param.20, bf16[1024,5120]{1,0:T(8,128)(2,1)} %param.12, f32[5120]{0:T(1024)S(1)} %copy-done.5, f32[1024]{0:T(1024)S(1)} %add_rsqrt_fusion), kind=kOutput, calls=%fused_computation.21 | convolution fusion | flops 85970649088 | bytes 144728064 | tf_op jit(solution)/shard_map/dot_general | solution.py:33
  262.2 2.5 copy.33
  266.3 181.8 %while.11 = (s32[]{:T(128)}, bf16[32,128,1,2,128]{4,1,0,3,2:T(8,128)(2,1)}, s32[32]{0:T(128)S(1)}, bf16[4096,2,128]{2,0,1:T(8,128)(2,1)}, bf16[4096,1,128]{2,0,1...) while((s32[]{:T(128)}, ...), condition=%wide.region_4.5_spmd.clone, body=%wide.region_1.4_spmd.clone.sunk | while | flops 544800384 | bytes 15866035 | solution.py:57
  273.6 1.8 fusion.68
  296.3 1.8 fusion.68
  353.1 1.8 fusion.68
  448.1 6.1 copy.35
  454.2 4.4 all-to-all-start.1
  458.7 97.9 %fusion.45 = f32[1024,5120]{1,0:T(8,128)} fusion(bf16[1024,8192]{1,0:T(8,128)(2,1)} %multiply_convert_fusion, bf16[8192,5120]{1,0:T(8,128)(2,1)} %param.21), kind=kOutput, calls=%fused_computation.47 | convolution fusion | flops 85899345920 | bytes 121634816 | tf_op jit(solution)/shard_map/dot_general | solution.py:35
  556.5 1.9 copy.36
  558.4 2.6 copy.37
  561.0 18.4 fusion.44
  579.4 1372.9 %all-reduce.3.cloned.1.call-done = (f32[1024,5120]{1,0:T(8,128)}, f32[1024,5120]{1,0:T(8,128)}) async-done(((f32[1024,5120]{1,0:T(8,128)}, f32[1024,5120]{1,0:T(8,128)}), (f32[1024,5120]{1,0:T(8,128)}, f32[1024,5120]{1,0:T(8,128)})) %all-reduce.3.cloned.1.call-update) | async-done | bytes 41943056 | tf_op jit(solution)/shard_map/psum | solution.py:91
  1952.3 22.1 %fusion.33 = bf16[1024,5120]{1,0:T(8,128)(2,1)} fusion(f32[1024,5120]{1,0:T(8,128)} %get-tuple-element.67, f32[1024,5120]{1,0:T(8,128)} %get-tuple-element.68, bf16[1024,5120]{1,0:T(8,128)(2,1)} %param.12), kind=kLoop, calls=%fused_computation.29 | loop fusion | flops 20971520 | bytes 62914560 | tf_op jit(solution)/shard_map/convert_element_type | solution.py:92
  (219 shorter events, 159.6 us)
Async XLA Ops:
  7.2 7.4 copy-start
  7.2 7.8 copy-start.2
  7.2 7.8 copy-start.5
  59.6 202.6 %all-to-all-start = ((bf16[1024,4,4,128]{3,0,2,1:T(8,128)(2,1)}), bf16[1024,4,4,128]{3,0,2,1:T(8,128)(2,1)}, u32[]{:S(2)}, u32[]{:S(2)}) async-start(bf16[1024,4,4,128]{3,0,2,1:T(8,128)(2,1)} %pad_maximum_fusion), calls=%async_computation | async-start | bytes 8388608 | tf_op jit(solution)/shard_map/all_to_all | solution.py:83
  448.0 108.5 %copy-start.3 = (bf16[4096,1,128]{2,0,1:T(8,128)(2,1)}, bf16[4096,1,128]{2,0,1:T(8,128)(2,1)S(1)}, u32[]{:S(2)}) copy-start(bf16[4096,1,128]{2,0,1:T(8,128)(2,1)S(1)} %get-tuple-element.154) | copy-start | bytes 3145732
  448.1 108.5 %copy-start.4 = (bf16[4096,1,128]{2,0,1:T(8,128)(2,1)}, bf16[4096,1,128]{2,0,1:T(8,128)(2,1)S(1)}, u32[]{:S(2)}) copy-start(bf16[4096,1,128]{2,0,1:T(8,128)(2,1)S(1)} %get-tuple-element.155) | copy-start | bytes 3145732
  454.2 102.3 %all-to-all-start.1 = ((bf16[4096,2,128]{2,1,0:T(2,128)(2,1)}), bf16[4096,2,128]{2,1,0:T(2,128)(2,1)}, u32[]{:S(2)}, u32[]{:S(2)}) async-start(bf16[4096,2,128]{2,1,0:T(2,128)(2,1)} %copy.35), calls=%async_computation.1 | async-start | bytes 4194304 | tf_op jit(solution)/shard_map/all_to_all | solution.py:89
  458.6 1493.7 %all-reduce.3.cloned.1.call-start = ((), (), s32[]{:S(2)}) async-start(), calls=%async_computation.2 | async-start | bytes 83886080 | tf_op jit(solution)/shard_map/psum | solution.py:91
  1952.3 22.1 %copy-start.1 = (bf16[5120,256]{1,0:T(8,128)(2,1)S(1)}, bf16[5120,256]{1,0:T(8,128)(2,1)}, u32[]{:S(2)}) copy-start(bf16[5120,256]{1,0:T(8,128)(2,1)} %param.17) | copy-start | bytes 7864324
Sparse Core Ops, SparseCore 0:
  579.5 1372.7 all-reduce.2
where the time goes:
time: 1990 us; the launch traced here: 1980 us
  waiting for transfers between devices  1370 us (69%)
  matrix products  450 us (23%)
  other arithmetic  73.4 us (4%)
  local copies, waits for them, and re-layouts  39.3 us (2%)
  loops' own time  21.6 us (1%)
    psum x1, waiting for transfers between devices, layer_block(): mlp_sum = lax.psum(gated_mlp(normed, w_gate, w_up, w_down), 'tp')  1370 us
    dot_general x1, matrix products, gated_mlp(): up_acc = jnp.dot(normed, w_up, preferred_element_type=jnp.float32)  100 us
    dot_general x1, matrix products, gated_mlp(): return jnp.dot(hidden, w_down, preferred_element_type=jnp.float32)  97.9 us
    dot_general x1, matrix products, gated_mlp(): gate_acc = jnp.dot(normed, w_gate, preferred_element_type=jnp.float32)  97.1 us
    dot_general x32, matrix products, attend_tile(): jnp.einsum('qcgd,kcd->cgqk', q_tile, k_keys, preferred_element_type=jnp.f...  58.7 us
    dot_general x32, matrix products, attend_tile(): jnp.einsum('cgqk,kcd->qcgd', weights.astype(jnp.bfloat16), v_keys, prefer...  48.1 us
  transfers between devices with their start and end apart: 3, of which 1 were waited for; matrix products, arithmetic and copies ran while one was open for 15% of the time, Pallas kernels for 0%

commit v1 on v0

v1 whole, which is shorter than its diff:
```python
import functools

import jax
import jax.numpy as jnp
from jax import lax
from jax.experimental import pallas as pl
from jax.experimental.pallas import tpu as pltpu
from jax.sharding import PartitionSpec as P

HEAD_DIM = 128
EPS = 1e-6
ROPE_BASE = 500000.0
EXP2_SCALE = HEAD_DIM ** -0.5 * 1.4426950408889634
MESH = pl.DeviceIdType.MESH
F32 = jnp.float32
BF16 = jnp.bfloat16

SLOTS = 6
SENDS = 4
HOP = 4
BACK_HOP = 3


def block_of(size, most):
    return most if size % most == 0 else 128


def rope_tables(positions):
    inv_freq = ROPE_BASE ** (-(jnp.arange(HEAD_DIM // 2, dtype=F32) * (2.0 / HEAD_DIM)))
    angles = positions.astype(F32)[:, None] * inv_freq[None, :]
    return jnp.cos(angles)[:, None, :], jnp.sin(angles)[:, None, :]


def rotate(vectors, cos_tab, sin_tab):
    half_dim = HEAD_DIM // 2
    lower_part = vectors[..., :half_dim]
    upper_part = vectors[..., half_dim:]
    return jnp.concatenate([lower_part * cos_tab - upper_part * sin_tab, upper_part * cos_tab + lower_part * sin_tab], axis=-1).astype(BF16)


def rms_norm(x_in, gain):
    x_f32 = x_in.astype(F32)
    inv_rms = lax.rsqrt(jnp.mean(x_f32 * x_f32, axis=-1, keepdims=True) + EPS)
    return (x_f32 * inv_rms * gain).astype(BF16)


def silu_mul(gate, up):
    return (gate / (1.0 + jnp.exp(-gate)) * up).astype(BF16)


def norm_rows(src_ref, gain_ref, dst_ref, dst_row, rows):
    step = 16
    gain = gain_ref[...]

    def body(i, carry):
        base = pl.multiple_of(i * step, step)
        dst_ref[pl.ds(pl.multiple_of(dst_row + base, step), step), :] = rms_norm(src_ref[pl.ds(base, step), :], gain)
        return carry

    lax.fori_loop(0, rows // step, body, 0)


def first_hidden_kernel(core_ref, u_ref, xp_ref, gain_ref, wg_ref, wu_ref, h_ref, ubuf):
    rows = u_ref.shape[0]
    core = core_ref[0]

    @pl.when(pl.program_id(0) == 0)
    def _():
        ubuf[pl.ds(pl.multiple_of(core * rows, rows), rows), :] = u_ref[...]
        norm_rows(xp_ref, gain_ref, ubuf, (1 - core) * rows, rows)

    gate = jnp.dot(ubuf[...], wg_ref[...], preferred_element_type=F32)
    up = jnp.dot(ubuf[...], wu_ref[...], preferred_element_type=F32)
    h_ref[...] = silu_mul(gate, up)


def first_hidden(core, u_own, x_par, gain, w_gate, w_up, rows):
    model = u_own.shape[1]
    ff_half = w_gate.shape[1] // 2
    block = block_of(ff_half, 512)
    blocks = ff_half // block
    return pl.pallas_call(
        first_hidden_kernel,
        grid_spec=pltpu.PrefetchScalarGridSpec(
            num_scalar_prefetch=1,
            grid=(blocks,),
            in_specs=[
                pl.BlockSpec((rows, model), lambda i, c: (0, 0)),
                pl.BlockSpec((rows, model), lambda i, c: (0, 0)),
                pl.BlockSpec((1, model), lambda i, c: (0, 0)),
                pl.BlockSpec((model, block), lambda i, c: (0, c[0] * blocks + i)),
                pl.BlockSpec((model, block), lambda i, c: (0, c[0] * blocks + i)),
            ],
            out_specs=pl.BlockSpec((2 * rows, block), lambda i, c: (0, i)),
            scratch_shapes=[pltpu.VMEM((2 * rows, model), BF16)],
        ),
        out_shape=jax.ShapeDtypeStruct((2 * rows, ff_half), BF16),
        compiler_params=pltpu.CompilerParams(vmem_limit_bytes=56 * 2 ** 20),
        cost_estimate=pl.CostEstimate(flops=8 * rows * model * ff_half, bytes_accessed=4 * model * ff_half, transcendentals=0),
        name="first_hidden",
    )(core, u_own, x_par, gain, w_gate, w_up)


def layer_kernel(
    rows, kb_rows,
    u_own, x_own, x_par, gain_ref, q_own, q_par, kv0, kv1, kv2, kv3, h0, w_gate, w_up, w_down, w_o,
    y_out,
    wg_buf, wu_buf, wd_buf, wo_buf, ubuf, xpbuf, hbuf, abuf, qbuf, kvbuf, pbuf, rbuf, xbuf, ybuf, gbuf, m_buf, l_buf, acc_buf,
    wg_sem, wu_sem, wd_sem, wo_sem, u_sem, xp_sem, q_sem, kv_sem, h0_sem, h_send, h_recv, a_send, a_recv,
    rs_send, rs_recv, x_sem, y_near, y_far, ag_recv, ag_send, credit,
):
    tokens, model = u_own.shape
    units = tokens // rows
    ff_half = w_gate.shape[1] // 2
    cols_half = model // 2
    bg = wg_buf.shape[2]
    bw = wd_buf.shape[2]
    nbg = ff_half // bg
    nbw = cols_half // bw
    q_cols = q_own.shape[1]
    heads = q_cols // HEAD_DIM
    per_unit = 2 * nbw
    pieces = per_unit * units
    unit_ticks = 2 * nbg + 2 + 2 * nbw

    z = lax.axis_index("tp")
    nz = lax.axis_size("tp")
    sp = lax.axis_index("sp")
    core = sp % 2
    row_y = sp // 2
    partner = sp + 1 - 2 * core
    step_z = 1 - 2 * core
    hop = jnp.where(core == 0, z, nz - 1 - z)
    z_next = jnp.clip(z + step_z, 0, nz - 1)
    z_prev = jnp.clip(z - step_z, 0, nz - 1)

    barrier = pltpu.get_barrier_semaphore()
    pl.semaphore_signal(barrier, inc=1, device_id={"sp": partner}, device_id_type=MESH)

    @pl.when(z > 0)
    def _():
        pl.semaphore_signal(barrier, inc=1, device_id={"tp": z - 1}, device_id_type=MESH)
        pl.semaphore_signal(barrier, inc=1, device_id={"tp": z - 1, "sp": partner}, device_id_type=MESH)

    @pl.when(z < nz - 1)
    def _():
        pl.semaphore_signal(barrier, inc=1, device_id={"tp": z + 1}, device_id_type=MESH)
        pl.semaphore_signal(barrier, inc=1, device_id={"tp": z + 1, "sp": partner}, device_id_type=MESH)

    def mult(value, of):
        return pl.multiple_of(value, of)

    def gate_up_copies(n):
        cols = pl.ds(mult(core * ff_half + n * bg, bg), bg)
        slot = n % 2
        return (
            pltpu.make_async_copy(w_gate.at[:, cols], wg_buf.at[slot], wg_sem.at[slot]),
            pltpu.make_async_copy(w_up.at[:, cols], wu_buf.at[slot], wu_sem.at[slot]),
        )

    def start_gate_up(n):
        for copy in gate_up_copies(n):
            copy.start()

    def down_copy(n):
        b, k = n // 2, n % 2
        half = jnp.where(k == 0, core, 1 - core)
        src = w_down.at[pl.ds(mult(half * ff_half, ff_half), ff_half), pl.ds(mult(core * cols_half + b * bw, bw), bw)]
        return pltpu.make_async_copy(src, wd_buf.at[k], wd_sem.at[k])

    def out_copy(b):
        return pltpu.make_async_copy(w_o.at[:, pl.ds(mult(core * cols_half + b * bw, bw), bw)], wo_buf.at[b % 2], wo_sem.at[b % 2])

    def u_copy(u):
        return pltpu.make_async_copy(
            u_own.at[pl.ds(mult(u * rows, rows), rows), :], ubuf.at[pl.ds(mult(core * rows, rows), rows), :], u_sem)

    def xp_copy(u):
        return pltpu.make_async_copy(x_par.at[pl.ds(mult(u * rows, rows), rows), :], xpbuf, xp_sem)

    def start_q(u):
        src = pl.ds(mult(u * rows, rows), rows)
        pltpu.make_async_copy(q_own.at[src, :], qbuf.at[core], q_sem.at[0]).start()
        pltpu.make_async_copy(q_par.at[src, :], qbuf.at[1 - core], q_sem.at[1]).start()

    def wait_q():
        src = pl.ds(0, rows)
        pltpu.make_async_copy(q_own.at[src, :], qbuf.at[core], q_sem.at[0]).wait()
        pltpu.make_async_copy(q_par.at[src, :], qbuf.at[1 - core], q_sem.at[1]).wait()

    def kv_copies():
        out = []
        for d, src in enumerate((kv0, kv1, kv2, kv3)):
            source = [sp, partner, 2 * (1 - row_y) + core, 2 * (1 - row_y) + 1 - core][d]
            out.append(pltpu.make_async_copy(src, kvbuf.at[pl.ds(mult(source * tokens, tokens), tokens), :], kv_sem.at[d]))
        return out

    def h_copy(u, j):
        view = hbuf.at[u % 2, :, pl.ds(mult(core * ff_half + j * bg, bg), bg)]
        return pltpu.make_async_remote_copy(view, view, h_send.at[j], h_recv.at[u % 2, j], device_id={"sp": partner}, device_id_type=MESH)

    def h0_copy(j):
        view = hbuf.at[0, :, pl.ds(mult(core * ff_half + j * bg, bg), bg)]
        return pltpu.make_async_remote_copy(
            h0.at[:, pl.ds(mult(j * bg, bg), bg)], view, h_send.at[j], h_recv.at[0, j], device_id={"sp": partner}, device_id_type=MESH)

    def a_copy(u):
        view = abuf.at[u % 2, :, pl.ds(mult(core * q_cols, q_cols), q_cols)]
        return pltpu.make_async_remote_copy(view, view, a_send, a_recv.at[u % 2], device_id={"sp": partner}, device_id_type=MESH)

    def part(p):
        u, i = p // per_unit, p % per_unit
        return u, i // 2, i % 2

    def sum_view(p):
        u, b, r = part(p)
        return pbuf.at[u % 2, pl.ds(mult(r * rows, rows), rows), pl.ds(mult(b * bw, bw), bw)]

    def sum_copy(p):
        return pltpu.make_async_remote_copy(
            sum_view(p), rbuf.at[p % SLOTS], rs_send.at[p % SENDS], rs_recv.at[p % SLOTS], device_id={"tp": z_next}, device_id_type=MESH)

    def y_view(owner, p):
        u, b, _ = part(p)
        return y_out.at[pl.ds(mult(u * rows, rows), rows), pl.ds(mult(owner * cols_half + b * bw, bw), bw)]

    def start_x(p):
        u, b, r = part(p)
        src = (pl.ds(mult(u * rows, rows), rows), pl.ds(mult(core * cols_half + b * bw, bw), bw))

        @pl.when(r == core)
        def _():
            pltpu.make_async_copy(x_own.at[src[0], src[1]], xbuf.at[p % SENDS], x_sem.at[p % SENDS]).start()

        @pl.when(r != core)
        def _():
            pltpu.make_async_copy(x_par.at[src[0], src[1]], xbuf.at[p % SENDS], x_sem.at[p % SENDS]).start()

    def near_local(p):
        return pltpu.make_async_copy(ybuf.at[p % SENDS], y_view(core, p), y_near.at[p % SENDS])

    def near_remote(p):
        return pltpu.make_async_remote_copy(
            ybuf.at[p % SENDS], y_view(core, p), y_near.at[p % SENDS], ag_recv.at[core, p // 2], device_id={"sp": partner}, device_id_type=MESH)

    def far_remote(p):
        _, _, r = part(p)
        return pltpu.make_async_remote_copy(
            ybuf.at[p % SENDS], y_view(core, p), y_far.at[p % SENDS], ag_recv.at[core, p // 2],
            device_id={"tp": z_prev, "sp": 2 * row_y + r}, device_id_type=MESH)

    def wait_result_out(p):
        near_local(p).wait()
        far_remote(p).wait_send()

    def back_copy(owner, q):
        view = y_view(owner, 2 * q)
        z_to = jnp.clip(z - 1 + 2 * owner, 0, nz - 1)
        return pltpu.make_async_remote_copy(view, view, ag_send.at[owner, q], ag_recv.at[owner, q], device_id={"tp": z_to}, device_id_type=MESH)

    def sum_op(p):
        view = sum_view(p)

        @pl.when(hop > 0)
        def _():
            sum_copy(p).wait_recv()
            u, b, r = part(p)
            at = (u % 2, pl.ds(mult(r * rows, rows), rows), pl.ds(mult(b * bw, bw), bw))
            pbuf[at] = pbuf[at] + rbuf[p % SLOTS]

            @pl.when(p + SLOTS < pieces)
            def _():
                pl.semaphore_signal(credit, inc=1, device_id={"tp": z_prev}, device_id_type=MESH)

        @pl.when(hop < nz - 1)
        def _():
            @pl.when(p >= SENDS)
            def _():
                sum_copy(p - SENDS).wait_send()

            @pl.when(p >= SLOTS)
            def _():
                pl.semaphore_wait(credit, 1)

            sum_copy(p).start()

        @pl.when(hop == nz - 1)
        def _():
            @pl.when(p >= SENDS)
            def _():
                wait_result_out(p - SENDS)

            slot = p % SENDS
            pltpu.make_async_copy(x_own.at[pl.ds(0, rows), pl.ds(0, bw)], xbuf.at[slot], x_sem.at[slot]).wait()
            ybuf[slot] = (xbuf[slot].astype(F32) + view[...]).astype(BF16)

            @pl.when(p + 2 < pieces)
            def _():
                start_x(p + 2)

            far_remote(p).start()
            r = p % 2

            @pl.when(r == core)
            def _():
                near_local(p).start()

            @pl.when(r != core)
            def _():
                near_remote(p).start()

    def back_op(owner, q, distance):
        back_copy(owner, q).wait_recv()

        @pl.when((distance > 0) & (distance < nz - 1))
        def _():
            back_copy(owner, q).start()

    def piece_at(v):
        v_ok = jnp.maximum(v, 0)
        p = (per_unit * v_ok + unit_ticks - 1) // unit_ticks
        return p, (v >= 0) & ((unit_ticks * p) // per_unit == v_ok) & (p < pieces)

    def tick(t):
        p, here = piece_at(t - 1 - hop * HOP)

        @pl.when(here)
        def _():
            sum_op(p)

        for owner in (0, 1):
            distance = nz - 1 - z if owner == 0 else z
            pb, back = piece_at(t - 2 - (nz - 1) * HOP - distance * BACK_HOP)
            mine = (distance == 0) & (core == owner)

            @pl.when(back & (pb % 2 == core) & jnp.logical_not(mine))
            def _():
                back_op(owner, pb // 2, distance)

    last_tick = (unit_ticks * (pieces - 1)) // per_unit + 2 + (nz - 1) * (HOP + BACK_HOP)

    def attend(u, r):
        token = (2 * row_y + r) * tokens + u * rows
        q_rows = qbuf[r]
        q_stack = jnp.concatenate([q_rows[:, i * HEAD_DIM:(i + 1) * HEAD_DIM] for i in range(heads)], axis=0)
        m_buf[...] = jnp.full_like(m_buf, -jnp.inf)
        l_buf[...] = jnp.zeros_like(l_buf)
        acc_buf[...] = jnp.zeros_like(acc_buf)

        def step(kb, masked):
            base = mult(kb * kb_rows, kb_rows)
            keys = kvbuf[pl.ds(base, kb_rows), :HEAD_DIM]
            values = kvbuf[pl.ds(base, kb_rows), HEAD_DIM:]
            s = lax.dot_general(q_stack, keys, (((1,), (1,)), ((), ())), preferred_element_type=F32)
            if masked:
                row_id = token + lax.broadcasted_iota(jnp.int32, s.shape, 0) % rows
                col_id = base + lax.broadcasted_iota(jnp.int32, s.shape, 1)
                s = jnp.where(col_id <= row_id, s, -jnp.inf)
            m_old = m_buf[...]
            m_new = jnp.maximum(m_old, jnp.max(s, axis=1, keepdims=True))
            m_buf[...] = m_new
            fade = jnp.exp2((m_old - m_new) * EXP2_SCALE)
            w = jnp.exp2((s - m_new[:, :1]) * EXP2_SCALE)
            total = w[:, :128]
            for i in range(1, kb_rows // 128):
                total = total + w[:, i * 128:(i + 1) * 128]
            l_buf[...] = l_buf[...] * fade + total
            acc_buf[...] = acc_buf[...] * fade + jnp.dot(w.astype(BF16), values, preferred_element_type=F32)

        last = token // kb_rows

        def body(kb, carry):
            step(kb, False)
            return carry

        lax.fori_loop(0, last, body, 0)
        step(last, True)
        out = (acc_buf[...] / jnp.sum(l_buf[...], axis=1, keepdims=True)).astype(BF16)
        for i in range(heads):
            abuf[u % 2, pl.ds(mult(r * rows, rows), rows), pl.ds(mult(core * q_cols + i * HEAD_DIM, HEAD_DIM), HEAD_DIM)] = out[i * rows:(i + 1) * rows]

    down_copy(0).start()
    out_copy(0).start()
    down_copy(1).start()
    out_copy(1).start()
    for copy in kv_copies():
        copy.start()
    start_q(0)
    own_h0 = pltpu.make_async_copy(h0, hbuf.at[0, :, pl.ds(mult(core * ff_half, ff_half), ff_half)], h0_sem)
    own_h0.start()

    @pl.when(hop == nz - 1)
    def _():
        start_x(0)
        start_x(1)

    pl.semaphore_wait(barrier, 1 + 2 * (z > 0).astype(jnp.int32) + 2 * (z < nz - 1).astype(jnp.int32))

    def send_h0(j, carry):
        h0_copy(j).start()
        return carry

    lax.fori_loop(0, nbg, send_h0, 0)
    own_h0.wait()
    for copy in kv_copies():
        copy.wait()

    def unit(u, carry):
        t0 = u * unit_ticks

        @pl.when(u > 0)
        def _():
            down_copy(0).start()
            out_copy(0).start()
            down_copy(1).start()
            out_copy(1).start()
            xp_copy(u).wait()
            norm_rows(xpbuf, gain_ref, ubuf, (1 - core) * rows, rows)
            u_copy(u).wait()

            def gate_up(n, carry):
                slot = n % 2
                copy_g, copy_u = gate_up_copies(n)
                copy_g.wait()
                gbuf[...] = jnp.dot(ubuf[...], wg_buf[slot], preferred_element_type=F32)
                tick(t0 - 2 - 2 * nbg + 2 * n)
                copy_u.wait()
                up = jnp.dot(ubuf[...], wu_buf[slot], preferred_element_type=F32)
                hbuf[u % 2, :, pl.ds(mult(core * ff_half + n * bg, bg), bg)] = silu_mul(gbuf[...], up)

                @pl.when(n + 2 < nbg)
                def _():
                    start_gate_up(n + 2)

                tick(t0 - 2 - 2 * nbg + 2 * n + 1)
                h_copy(u, n).start()
                return carry

            lax.fori_loop(0, nbg, gate_up, 0)

        wait_q()

        def half(r, carry):
            attend(u, r)

            @pl.when(u > 0)
            def _():
                tick(t0 - 2 + r)

            return carry

        lax.fori_loop(0, 2, half, 0)
        a_copy(u).start()

        @pl.when(u + 1 < units)
        def _():
            start_q(u + 1)
            u_copy(u + 1).start()
            xp_copy(u + 1).start()
            start_gate_up(0)
            start_gate_up(1)

        def wait_h(j, carry):
            h_copy(u, j).wait()
            return carry

        def down(b, carry):
            cols = pl.ds(mult(b * bw, bw), bw)
            own_rows = pl.ds(mult(core * ff_half, ff_half), ff_half)
            par_rows = pl.ds(mult((1 - core) * ff_half, ff_half), ff_half)
            down_copy(2 * b).wait()
            pbuf[u % 2, :, cols] = jnp.dot(hbuf[u % 2, :, own_rows], wd_buf[0], preferred_element_type=F32)

            @pl.when(b + 1 < nbw)
            def _():
                down_copy(2 * b + 2).start()

            tick(t0 + 2 * b)

            @pl.when(b == 0)
            def _():
                lax.fori_loop(0, nbg, wait_h, 0)
                a_copy(u).wait()

            down_copy(2 * b + 1).wait()
            out_copy(b).wait()
            pbuf[u % 2, :, cols] = (
                pbuf[u % 2, :, cols]
                + jnp.dot(hbuf[u % 2, :, par_rows], wd_buf[1], preferred_element_type=F32)
                + jnp.dot(abuf[u % 2], wo_buf[b % 2], preferred_element_type=F32)
            )

            @pl.when(b + 1 < nbw)
            def _():
                down_copy(2 * b + 3).start()

            @pl.when(b + 2 < nbw)
            def _():
                out_copy(b + 2).start()

            tick(t0 + 2 * b + 1)
            return carry

        lax.fori_loop(0, nbw, down, 0)
        return carry

    lax.fori_loop(0, units, unit, 0)

    def drain(t, carry):
        tick(t)
        return carry

    lax.fori_loop((units - 1) * unit_ticks + 2 * nbw, last_tick + 1, drain, 0)

    def sums_out(i, carry):
        p = pieces - SENDS + i

        @pl.when(hop < nz - 1)
        def _():
            sum_copy(p).wait_send()

        @pl.when(hop == nz - 1)
        def _():
            wait_result_out(p)

        return carry

    lax.fori_loop(0, SENDS, sums_out, 0)

    for owner in (0, 1):
        distance = nz - 1 - z if owner == 0 else z

        @pl.when((distance > 0) & (distance < nz - 1))
        def _():
            def backs_out(q, carry):
                back_copy(owner, q).wait_send()
                return carry

            lax.fori_loop(0, pieces // 2, backs_out, 0)


def layer(u_own, x_own, x_par, gain, q_own, q_par, kvs, h0, w_gate, w_up, w_down, w_o, rows):
    tokens, model = u_own.shape
    ff = w_gate.shape[1]
    ff_half, cols_half = ff // 2, model // 2
    bg, bw = block_of(ff_half, 512), block_of(cols_half, 512)
    nbg, nbw = ff_half // bg, cols_half // bw
    q_cols = q_own.shape[1]
    kv_tokens = 4 * tokens
    kb_rows = min(512, kv_tokens // 2)
    pieces = 2 * nbw * (tokens // rows)
    stack = rows * (q_cols // HEAD_DIM)
    any_spec = pl.BlockSpec(memory_space=pl.ANY)
    dma = pltpu.SemaphoreType.DMA
    macs = 2 * tokens * ff_half * model * 2 + 2 * tokens * ff * cols_half + 2 * tokens * w_o.shape[0] * cols_half
    return pl.pallas_call(
        functools.partial(layer_kernel, rows, kb_rows),
        out_shape=jax.ShapeDtypeStruct((tokens, model), BF16),
        in_specs=[any_spec] * 3 + [pl.BlockSpec(memory_space=pltpu.VMEM)] + [any_spec] * 11,
        out_specs=any_spec,
        scratch_shapes=[
            pltpu.VMEM((2, model, bg), BF16),
            pltpu.VMEM((2, model, bg), BF16),
            pltpu.VMEM((2, ff_half, bw), BF16),
            pltpu.VMEM((2, w_o.shape[0], bw), BF16),
            pltpu.VMEM((2 * rows, model), BF16),
            pltpu.VMEM((rows, model), BF16),
            pltpu.VMEM((2, 2 * rows, ff), BF16),
            pltpu.VMEM((2, 2 * rows, w_o.shape[0]), BF16),
            pltpu.VMEM((2, rows, q_cols), BF16),
            pltpu.VMEM((kv_tokens, 2 * HEAD_DIM), BF16),
            pltpu.VMEM((2, 2 * rows, cols_half), F32),
            pltpu.VMEM((SLOTS, rows, bw), F32),
            pltpu.VMEM((SENDS, rows, bw), BF16),
            pltpu.VMEM((SENDS, rows, bw), BF16),
            pltpu.VMEM((2 * rows, bg), F32),
            pltpu.VMEM((stack, 128), F32),
            pltpu.VMEM((stack, 128), F32),
            pltpu.VMEM((stack, HEAD_DIM), F32),
            dma((2,)), dma((2,)), dma((2,)), dma((2,)), dma, dma, dma((2,)), dma((4,)), dma,
            dma((nbg,)), dma((2, nbg)), dma, dma((2,)),
            dma((SENDS,)), dma((SLOTS,)), dma((SENDS,)), dma((SENDS,)), dma((SENDS,)),
            dma((2, pieces // 2)), dma((2, pieces // 2)),
            pltpu.SemaphoreType.REGULAR,
        ],
        compiler_params=pltpu.CompilerParams(
            collective_id=0, has_side_effects=True, vmem_limit_bytes=67043328),
        cost_estimate=pl.CostEstimate(flops=2 * macs, bytes_accessed=6 * ff_half * model * (tokens // rows), transcendentals=0),
        name="layer",
    )(u_own, x_own, x_par, gain, q_own, q_par, *kvs, h0, w_gate, w_up, w_down, w_o)


def solution(mesh):
    row_spec = P(("rep", "sp"), None)
    cache_spec = P("rep", ("tp", "sp"), None)
    other_core = [(0, 1), (1, 0), (2, 3), (3, 2)]
    other_chip = [(0, 2), (2, 0), (1, 3), (3, 1)]
    other_both = [(0, 3), (3, 0), (1, 2), (2, 1)]

    def layer_block(x_in, positions, norm_gain, w_q, w_k, w_v, w_o, w_gate, w_up, w_down):
        tokens = x_in.shape[0]
        rows = 128 if tokens >= 1024 else tokens // 4
        heads_tp = w_q.shape[1] // HEAD_DIM
        kv_tp = w_k.shape[1] // HEAD_DIM
        core = lax.axis_index("sp") % 2
        core_arr = core.astype(jnp.int32).reshape(1)
        gain = norm_gain.reshape(1, -1)

        x_par = lax.ppermute(x_in, "sp", other_core)
        normed = rms_norm(x_in, norm_gain)
        cos_tab, sin_tab = rope_tables(positions)
        k_rot = rotate(jnp.dot(normed, w_k, preferred_element_type=F32).reshape(tokens, kv_tp, HEAD_DIM), cos_tab, sin_tab)
        v_val = jnp.dot(normed, w_v, preferred_element_type=F32).astype(BF16).reshape(tokens, kv_tp, HEAD_DIM)
        kv = jnp.concatenate([k_rot, v_val], axis=2)
        kv_mine = lax.dynamic_index_in_dim(kv, core, 1, keepdims=False)
        kv_other = lax.dynamic_index_in_dim(kv, 1 - core, 1, keepdims=False)
        kv_c = lax.ppermute(kv_mine, "sp", other_chip)
        kv_d = lax.ppermute(kv_other, "sp", other_both)
        kv_b = lax.ppermute(kv_other, "sp", other_core)
        q_rot = rotate(jnp.dot(normed, w_q, preferred_element_type=F32).reshape(tokens, heads_tp, HEAD_DIM), cos_tab, sin_tab)
        q_rot = q_rot.reshape(tokens, 2, heads_tp // 2 * HEAD_DIM)
        q_mine = lax.dynamic_index_in_dim(q_rot, core, 1, keepdims=False)
        q_other = lax.dynamic_index_in_dim(q_rot, 1 - core, 1, keepdims=False)
        q_par = lax.ppermute(q_other, "sp", other_core)

        h0 = first_hidden(core_arr, normed, x_par, gain, w_gate, w_up, rows)
        kv_late, h0 = lax.optimization_barrier((kv, h0))
        cache = lax.all_to_all(jnp.repeat(kv_late, 2, axis=1), "sp", 1, 0, tiled=True)
        y_out = layer(normed, x_in, x_par, gain, q_mine, q_par, (kv_mine, kv_b, kv_c, kv_d), h0, w_gate, w_up, w_down, w_o, rows)
        return y_out, cache[..., :HEAD_DIM], cache[..., HEAD_DIM:]

    return jax.shard_map(
        layer_block,
        mesh=mesh,
        in_specs=(row_spec, P(("rep", "sp")), P(None), P(None, "tp"), P(None, "tp"), P(None, "tp"), P("tp", None), P(None, "tp"), P(None, "tp"), P("tp", None)),
        out_specs=(row_spec, cache_spec, cache_spec),
        check_vma=False,
    )
```

time: 1990 us -> 675 us (0.34)
  waiting for transfers between devices: 1370 us -> 0.02 us
  Pallas kernels: 0 us -> 597 us
  matrix products: 450 us -> 29.3 us
  other arithmetic: 73.4 us -> 17.3 us
  loops' own time: 21.6 us -> 0 us
    psum x1 -> x0, waiting for transfers between devices: 1370 us -> none  [layer_block(): mlp_sum = lax.psum(gated_mlp(normed, w_gate, w_up, w_down), 'tp')]
    pallas_call x0 -> x2, Pallas kernels: none -> 597 us  [the longest x1 562 us: layer(): pl.pallas_call(functools.partial(layer_kernel, rows, kb_rows), out_shape=...]
    dot_general x71 -> x3, matrix products: 450 us -> 29.3 us  [the longest x1 16.1 us: layer_block(): jnp.dot(normed, w_q, preferred_element_type=F32)]
    reduce_sum x32 -> x0, other arithmetic: 23 us -> none  [attend_tile(): weight_total = jnp.sum(weights, axis=-1)]
    another operation x1 -> x0, loops' own time: 21.6 us -> none  [causal_attention(): attn_tiles = lax.map(attend_tile, jnp.arange(tokens_q // tile_rows))]
  transfers between devices with their start and end apart: 3 -> 6, of which waited for: 1 -> 0; matrix products, arithmetic and copies ran while one was open for 15% -> 8% of each run, Pallas kernels for 0% -> 89%
where the time goes in v1:
time: 675 us; the launch traced here: 673 us
  Pallas kernels  597 us (88%)
  matrix products  29.3 us (4%)
  local copies, waits for them, and re-layouts  22 us (3%)
  other arithmetic  17.3 us (3%)
  starting transfers between devices  7.41 us (1%)
    pallas_call x1, Pallas kernels, layer(): pl.pallas_call(functools.partial(layer_kernel, rows, kb_rows), out_shape=...  562 us
    pallas_call x1, Pallas kernels, first_hidden(): pl.pallas_call(first_hidden_kernel, grid_spec=pltpu.PrefetchScalarGridSpe...  34.7 us
    dot_general x1, matrix products, layer_block(): jnp.dot(normed, w_q, preferred_element_type=F32)  16.1 us
  transfers between devices with their start and end apart: 6, of which 0 were waited for; matrix products, arithmetic and copies ran while one was open for 8% of the time, Pallas kernels for 89%

profile of v1, /device:TPU:5, one launch (start us, length us, event | category | flops | bytes accessed | tf_op | source)
XLA Modules:
  0.0 673.4 jit_solution(17848610931148759051)
XLA Ops:
  0.6 0.7 collective-permute-start
  1.4 0.7 convert_element_type.20
  2.1 1.0 multiply_cosine_fusion
  3.1 1.0 copy.21
  4.1 1.0 copy.23
  5.1 6.1 fusion
  11.2 6.7 fusion.2.u_ref.u_own
  17.9 6.7 convolution_convert_fusion
  24.9 6.5 fusion.6
  31.3 0.9 fusion.4
  32.6 1.4 copy.25
  34.0 1.5 subtract_convert_fusion.1
  35.9 1.1 dynamic-slice_bitcast_fusion
  37.0 1.8 collective-permute-start.3
  38.9 16.1 %fusion.5 = f32[1024,1024]{0,1:T(8,128)S(1)} fusion(bf16[1024,5120]{1,0:T(8,128)(2,1)} %copy-done, bf16[5120,1024]{1,0:T(8,128)(2,1)} %param.13), kind=kOutput, calls=%fused_computation.22 | convolution fusion | flops 10737418240 | bytes 25165824 | tf_op jit(solution)/shard_map/dot_general | solution.py:620
  55.0 0.7 subtract_convert_fusion
  56.1 1.3 copy.19
  57.8 1.3 copy.18
  59.1 34.7 %first_hidden.1.h0 = bf16[256,4096]{1,0:T(8,128)(2,1)} custom-call(s32[1]{0:T(128)} %bitcast.9.core_ref, bf16[1024,5120]{1,0:T(8,128)(2,1)} %copy-done, bf16[1024,5120]{1,0:T(8,128)(2,1)} %collective-permute-done.xp_ref.x_par, f32[1,5120]{1,0:T(1,128)} %bitcast.30, bf16[5120,8192]{1,0:T(8,128)(2,1)} %w_gate.1, bf16[5120,8192]{1,0:T(8,128)(2,1)} %w_up.1), custom_call_target="tpu_custom_call" | custom-call | flops 21474836480 | bytes 83886080 | tf_op jit(solution)/shard_map/first_hidden/pallas_call | solution.py:82
  93.7 1.5 broadcast_in_dim.5
  95.2 4.5 all-to-all-start
  99.8 561.9 %layer.1 = bf16[1024,5120]{1,0:T(8,128)(2,1)} custom-call(bf16[1024,5120]{1,0:T(8,128)(2,1)} %copy-done, bf16[1024,5120]{1,0:T(8,128)(2,1)} %x_own.1, bf16[1024,5120]{1,0:T(8,128)(2,1)} %collective-permute-done.xp_ref.x_par, f32[1,5120]{1,0:T(1,128)} %bitcast.31, bf16[1024,512]{1,0:T(8,128)(2,1)} %bitcast.26, ...), custom_call_target="tpu_custom_call" | custom-call | flops 268435456000 | bytes 1006632960 | tf_op jit(solution)/shard_map/layer/pallas_call | solution.py:556
  661.6 3.0 fusion.3
  664.6 8.8 %copy.28 = bf16[1024,5120]{1,0:T(8,128)(2,1)} copy(bf16[1024,5120]{1,0:T(8,128)(2,1)} %layer.1) | data formatting | bytes 20971520
  (20 shorter events, 1.8 us)
Async XLA Ops:
  0.6 58.5 %collective-permute-start = (bf16[1024,5120]{1,0:T(8,128)(2,1)}, bf16[1024,5120]{1,0:T(8,128)(2,1)}, u32[]{:S(2)}, u32[]{:S(2)}) collective-permute-start(bf16[1024,5120]{1,0:T(8,128)(2,1)} %x_own.1), channel_id=1, source_target_pairs={{0,1},{1,0},{2,3},{3,2},{4,5},{5,4},{6,7},{7,6},{8,9},{9,8},{10,11... | collective-permute-start | bytes 31457288 | tf_op jit(solution)/shard_map/ppermute | solution.py:609
  5.1 6.1 copy-start.1
  17.9 6.7 copy-start
  37.0 62.7 %collective-permute-start.4 = (bf16[1024,256]{1,0:T(8,128)(2,1)}, bf16[1024,256]{1,0:T(8,128)(2,1)}, u32[]{:S(2)}, u32[]{:S(2)}) collective-permute-start(bf16[1024,256]{1,0:T(8,128)(2,1)} %get-tuple-element.15), channel_id=1, source_target_pairs={{0,3},{3,0},{1,2},{2,1},{4,7},{7,4},{5,6},{6,5},{8,11},{11,8},{9,1... | collective-permute-start | bytes 1572872 | tf_op jit(solution)/shard_map/ppermute | solution.py:618
  37.0 62.7 %collective-permute-start.2 = (bf16[1024,256]{1,0:T(8,128)(2,1)}, bf16[1024,256]{1,0:T(8,128)(2,1)}, u32[]{:S(2)}, u32[]{:S(2)}) collective-permute-start(bf16[1024,256]{1,0:T(8,128)(2,1)} %get-tuple-element.15), channel_id=1, source_target_pairs={{0,1},{1,0},{2,3},{3,2},{4,5},{5,4},{6,7},{7,6},{8,9},{9,8},{10,11... | collective-permute-start | bytes 1572872 | tf_op jit(solution)/shard_map/ppermute | solution.py:619
  37.0 62.7 %collective-permute-start.3 = (bf16[1024,256]{1,0:T(8,128)(2,1)}, bf16[1024,256]{1,0:T(8,128)(2,1)}, u32[]{:S(2)}, u32[]{:S(2)}) collective-permute-start(bf16[1024,256]{1,0:T(8,128)(2,1)} %get-tuple-element.16.kv0), channel_id=1, source_target_pairs={{0,2},{2,0},{1,3},{3,1},{4,6},{6,4},{5,7},{7,5},{8,10},{10,8},{9,1... | collective-permute-start | bytes 1572872 | tf_op jit(solution)/shard_map/ppermute | solution.py:617
  57.4 42.3 %collective-permute-start.1 = (bf16[1024,512]{1,0:T(8,128)(2,1)}, bf16[1024,512]{1,0:T(8,128)(2,1)}, u32[]{:S(2)}, u32[]{:S(2)}) collective-permute-start(bf16[1024,512]{1,0:T(8,128)(2,1)} %bitcast.27), channel_id=1, source_target_pairs={{0,1},{1,0},{2,3},{3,2},{4,5},{5,4},{6,7},{7,6},{8,9},{9,8},{10,11... | collective-permute-start | bytes 3145736 | tf_op jit(solution)/shard_map/ppermute | solution.py:624
  95.2 566.4 %all-to-all-start = ((bf16[1024,4,256]{2,0,1:T(8,128)(2,1)}), bf16[1024,4,256]{2,0,1:T(8,128)(2,1)}, u32[]{:S(2)}, u32[]{:S(2)}) async-start(bf16[1024,4,256]{2,0,1:T(8,128)(2,1)} %bitcast.10), calls=%async_computation | async-start | bytes 4194304 | tf_op jit(solution)/shard_map/all_to_all | solution.py:628

commit v2 on v1

v2 whole, which is shorter than its diff:
```python
import functools
import math

import jax
import jax.numpy as jnp
from jax import lax
from jax.experimental import pallas as pl
from jax.experimental.pallas import tpu as pltpu
from jax.sharding import PartitionSpec as P

HEAD_DIM = 128
EPS = 1e-6
ROPE_BASE = 500000.0
EXP2_SCALE = HEAD_DIM ** -0.5 * 1.4426950408889634
MESH = pl.DeviceIdType.MESH
F32 = jnp.float32
BF16 = jnp.bfloat16

SLOTS = 8
SENDS = 4
HOP = 4
BACK_HOP = 3
DOWN_SLOTS = 2


def block_of(size, most):
    return most if size % most == 0 else most // 2


def over(x, d):
    if d & (d - 1) == 0:
        return lax.shift_right_logical(x, d.bit_length() - 1)
    return lax.shift_right_logical(x * (65536 // d + 1), 16)


def rope_tables(positions):
    inv_freq = ROPE_BASE ** (-(jnp.arange(HEAD_DIM // 2, dtype=F32) * (2.0 / HEAD_DIM)))
    angles = positions.astype(F32)[:, None] * jnp.concatenate([inv_freq, inv_freq])[None, :]
    sign = jnp.where(jnp.arange(HEAD_DIM) < HEAD_DIM // 2, -1.0, 1.0)
    return jnp.cos(angles), jnp.sin(angles) * sign[None, :]


def rotate(vectors, cos_tab, sin_tab):
    return (vectors * cos_tab + pltpu.roll(vectors, HEAD_DIM // 2, 1) * sin_tab).astype(BF16)


def rms_norm(x_in, gain):
    x_f32 = x_in.astype(F32)
    inv_rms = lax.rsqrt(jnp.mean(x_f32 * x_f32, axis=-1, keepdims=True) + EPS)
    return (x_f32 * inv_rms * gain).astype(BF16)


def silu_mul(gate, up):
    return (gate / (1.0 + jnp.exp(-gate)) * up).astype(BF16)


def qkv_kernel(core_ref, x_ref, gain_ref, cos_ref, sin_ref, wk_ref, wv_ref, wq_ref, u_ref, kv_ref, vt_ref, q_other_ref, q_mine_ref, u_buf):
    phase, block = pl.program_id(0), pl.program_id(1)
    rows = x_ref.shape[0]
    at = pl.ds(pl.multiple_of(block * rows, rows), rows)

    @pl.when(phase == 0)
    def _():
        step = 16

        def norm(i, carry):
            part = pl.ds(pl.multiple_of(i * step, step), step)
            u_ref[part, :] = rms_norm(x_ref[part, :], gain_ref[...])
            return carry

        lax.fori_loop(0, rows // step, norm, 0)
        u_buf[at, :] = u_ref[...]
        k = jnp.dot(u_ref[...], wk_ref[...], preferred_element_type=F32)
        v = jnp.dot(u_ref[...], wv_ref[...], preferred_element_type=F32)
        for head in range(2):
            cols = slice(head * HEAD_DIM, (head + 1) * HEAD_DIM)
            kv_ref[head, :, :HEAD_DIM] = rotate(k[:, cols], cos_ref[at, :], sin_ref[at, :])
            kv_ref[head, :, HEAD_DIM:] = v[:, cols].astype(BF16)
            vt_ref[head] = v[:, cols].T.astype(BF16)

    def queries(q_ref):
        q = jnp.dot(u_buf[at, :], wq_ref[...], preferred_element_type=F32)
        for head in range(q.shape[1] // HEAD_DIM):
            cols = slice(head * HEAD_DIM, (head + 1) * HEAD_DIM)
            q_ref[:, cols] = rotate(q[:, cols], cos_ref[at, :], sin_ref[at, :])

    pl.when(phase == 1)(lambda: queries(q_other_ref))
    pl.when(phase == 2)(lambda: queries(q_mine_ref))


def project(core, x_in, gain, cos_tab, sin_tab, w_k, w_v, w_q):
    tokens, model = x_in.shape
    rows = min(256, tokens // 2)
    blocks = tokens // rows
    q_cols = w_q.shape[1] // 2
    last = blocks - 1

    def first(p, i):
        return jnp.where(p == 0, i, last)

    return pl.pallas_call(
        qkv_kernel,
        grid_spec=pltpu.PrefetchScalarGridSpec(
            num_scalar_prefetch=1,
            grid=(3, blocks),
            in_specs=[
                pl.BlockSpec((rows, model), lambda p, i, c: (first(p, i), 0)),
                pl.BlockSpec((1, model), lambda p, i, c: (0, 0)),
                pl.BlockSpec((tokens, HEAD_DIM), lambda p, i, c: (0, 0)),
                pl.BlockSpec((tokens, HEAD_DIM), lambda p, i, c: (0, 0)),
                pl.BlockSpec((model, 2 * HEAD_DIM), lambda p, i, c: (0, 0)),
                pl.BlockSpec((model, 2 * HEAD_DIM), lambda p, i, c: (0, 0)),
                pl.BlockSpec((model, q_cols), lambda p, i, c: (0, jnp.where(p == 2, c[0], 1 - c[0]))),
            ],
            out_specs=[
                pl.BlockSpec((rows, model), lambda p, i, c: (first(p, i), 0)),
                pl.BlockSpec((2, rows, 2 * HEAD_DIM), lambda p, i, c: (0, first(p, i), 0)),
                pl.BlockSpec((2, HEAD_DIM, rows), lambda p, i, c: (0, 0, first(p, i))),
                pl.BlockSpec((rows, q_cols), lambda p, i, c: (jnp.where(p == 0, 0, jnp.where(p == 1, i, last)), 0)),
                pl.BlockSpec((rows, q_cols), lambda p, i, c: (jnp.where(p == 2, i, 0), 0)),
            ],
            scratch_shapes=[pltpu.VMEM((tokens, model), BF16)],
        ),
        out_shape=[
            jax.ShapeDtypeStruct((tokens, model), BF16),
            jax.ShapeDtypeStruct((2, tokens, 2 * HEAD_DIM), BF16),
            jax.ShapeDtypeStruct((2, HEAD_DIM, tokens), BF16),
            jax.ShapeDtypeStruct((tokens, q_cols), BF16),
            jax.ShapeDtypeStruct((tokens, q_cols), BF16),
        ],
        compiler_params=pltpu.CompilerParams(vmem_limit_bytes=60 * 2 ** 20),
        cost_estimate=pl.CostEstimate(flops=2 * tokens * model * (2 * q_cols + 4 * HEAD_DIM), bytes_accessed=6 * tokens * model, transcendentals=0),
        name="project",
    )(core, x_in, gain, cos_tab, sin_tab, w_k, w_v, w_q)


def layer_kernel(
    rows, att, keys_step,
    u_own, x_own, x_par, q_mine, q_other, kv, vt, w_gate, w_up, w_down, w_o,
    y_out, cache, u_par,
    wgu_buf, wd_buf, wo_buf, ubuf, hbuf, abuf, qbuf, kbuf, vtbuf, pbuf, rbuf, xbuf, ybuf, m_buf, l_buf, acc_buf,
    wgu_sem, wd_sem, wo_sem, u_sem, near_sem, u_send, u_recv, q_send, q_recv, kv_send, kv_recv,
    h_send, h_recv, a_send, a_recv, rs_send, rs_recv, x_sem, y_near, y_far, ag_recv, ag_send, credit,
):
    tokens, model = u_own.shape
    units = tokens // rows
    ff_half = w_gate.shape[1] // 2
    cols_half = model // 2
    bg = wgu_buf.shape[2] // 2
    wb = wd_buf.shape[2]
    bw = wb // 2
    nbg = ff_half // bg
    nbw = cols_half // bw
    q_cols = q_mine.shape[1]
    heads = q_cols // HEAD_DIM
    subs = rows // att
    per_unit = 2 * nbw
    pieces = per_unit * units
    unit_ticks = 2 * nbg + 2 * subs + 2 * nbw

    z = lax.axis_index("tp")
    nz = lax.axis_size("tp")
    sp = lax.axis_index("sp")
    core = sp % 2
    row_y = sp // 2
    partner = sp + 1 - 2 * core
    across = 2 * (1 - row_y) + core
    across_partner = 2 * (1 - row_y) + 1 - core
    step_z = 1 - 2 * core
    hop = jnp.where(core == 0, z, nz - 1 - z)
    z_next = jnp.clip(z + step_z, 0, nz - 1)
    z_prev = jnp.clip(z - step_z, 0, nz - 1)

    def mult(value, of):
        return pl.multiple_of(value, of)

    def gate_up_copies(n):
        cols = pl.ds(mult(core * ff_half + n * bg, bg), bg)
        slot = n & 1
        return (
            pltpu.make_async_copy(w_gate.at[:, cols], wgu_buf.at[slot, :, pl.ds(0, bg)], wgu_sem.at[slot, 0]),
            pltpu.make_async_copy(w_up.at[:, cols], wgu_buf.at[slot, :, pl.ds(bg, bg)], wgu_sem.at[slot, 1]),
        )

    def start_gate_up(n):
        for copy in gate_up_copies(n):
            copy.start()

    def down_copy(n):
        b, k = n // 2, n % 2
        half = jnp.where(k == 0, core, 1 - core)
        src = w_down.at[pl.ds(mult(half * ff_half, ff_half), ff_half), pl.ds(mult(core * cols_half + b * wb, wb), wb)]
        slot = n % DOWN_SLOTS
        return pltpu.make_async_copy(src, wd_buf.at[slot], wd_sem.at[slot])

    def out_copy(b):
        return pltpu.make_async_copy(w_o.at[:, pl.ds(mult(core * cols_half + b * wb, wb), wb)], wo_buf.at[b & 1], wo_sem.at[b & 1])

    def u_rows(u):
        return pl.ds(mult(u * rows, rows), rows)

    def own_u_copy(u):
        return pltpu.make_async_copy(u_own.at[u_rows(u), :], ubuf.at[u_rows(core), :], u_sem.at[0])

    def par_u_copy(u):
        return pltpu.make_async_copy(u_par.at[u_rows(u), :], ubuf.at[u_rows(1 - core), :], u_sem.at[1])

    own_tokens = pl.ds(mult(sp * tokens, tokens), tokens)

    def own_copies():
        return (
            pltpu.make_async_copy(q_mine, qbuf.at[core], near_sem.at[0]),
            pltpu.make_async_copy(kv.at[core, :, pl.ds(0, HEAD_DIM)], kbuf.at[own_tokens, :], near_sem.at[1]),
            pltpu.make_async_copy(vt.at[core], vtbuf.at[:, own_tokens], near_sem.at[2]),
        )

    def own_cache():
        return pltpu.make_async_copy(kv.at[row_y], cache.at[own_tokens, :], near_sem.at[3])

    def h_copy(u, j):
        view = hbuf.at[u & 1, :, pl.ds(mult(core * ff_half + j * bg, bg), bg)]
        return pltpu.make_async_remote_copy(view, view, h_send.at[j], h_recv.at[u & 1, j], device_id={"sp": partner}, device_id_type=MESH)

    def first_u_copy():
        return pltpu.make_async_remote_copy(
            u_own.at[u_rows(0), :], ubuf.at[u_rows(core), :], u_send.at[0], u_recv.at[0], device_id={"sp": partner}, device_id_type=MESH)

    def far_u_copy(u):
        return pltpu.make_async_remote_copy(
            u_own.at[u_rows(u), :], u_par.at[u_rows(u), :], u_send.at[u], u_recv.at[u], device_id={"sp": partner}, device_id_type=MESH)

    def q_copy():
        return pltpu.make_async_remote_copy(q_other, qbuf.at[core], q_send, q_recv, device_id={"sp": partner}, device_id_type=MESH)

    peers = ((partner, 1 - core, row_y), (across, core, 1 - row_y), (across_partner, 1 - core, 1 - row_y))

    def key_copies(d):
        to, head, _ = peers[d]
        return (
            pltpu.make_async_remote_copy(
                kv.at[head, :, pl.ds(0, HEAD_DIM)], kbuf.at[own_tokens, :], kv_send.at[0, d], kv_recv.at[0, d], device_id={"sp": to}, device_id_type=MESH),
            pltpu.make_async_remote_copy(
                vt.at[head], vtbuf.at[:, own_tokens], kv_send.at[1, d], kv_recv.at[1, d], device_id={"sp": to}, device_id_type=MESH),
        )

    def cache_copy(d):
        to, _, head = peers[d]
        return pltpu.make_async_remote_copy(
            kv.at[head], cache.at[own_tokens, :], kv_send.at[2, d], kv_recv.at[2, d], device_id={"sp": to}, device_id_type=MESH)

    def a_copy(u):
        view = abuf.at[u & 1, :, pl.ds(mult(core * q_cols, q_cols), q_cols)]
        return pltpu.make_async_remote_copy(view, view, a_send, a_recv.at[u & 1], device_id={"sp": partner}, device_id_type=MESH)

    def part(p):
        u = over(p, per_unit)
        i = p - u * per_unit
        return u, lax.shift_right_logical(i, 1), i & 1

    def sum_view(p):
        u, b, r = part(p)
        return pbuf.at[u & 1, pl.ds(mult(r * rows, rows), rows), pl.ds(mult(b * bw, bw), bw)]

    def sum_copy(p):
        return pltpu.make_async_remote_copy(
            sum_view(p), rbuf.at[p & (SLOTS - 1)], rs_send.at[p & (SENDS - 1)], rs_recv.at[p & (SLOTS - 1)], device_id={"tp": z_next}, device_id_type=MESH)

    def y_view(owner, p):
        u, b, _ = part(p)
        return y_out.at[pl.ds(mult(u * rows, rows), rows), pl.ds(mult(owner * cols_half + b * bw, bw), bw)]

    def start_x(p):
        u, b, r = part(p)
        src = (pl.ds(mult(u * rows, rows), rows), pl.ds(mult(core * cols_half + b * bw, bw), bw))

        @pl.when(r == core)
        def _():
            pltpu.make_async_copy(x_own.at[src[0], src[1]], xbuf.at[p & (SENDS - 1)], x_sem.at[p & (SENDS - 1)]).start()

        @pl.when(r != core)
        def _():
            pltpu.make_async_copy(x_par.at[src[0], src[1]], xbuf.at[p & (SENDS - 1)], x_sem.at[p & (SENDS - 1)]).start()

    def near_local(p):
        return pltpu.make_async_copy(ybuf.at[p & (SENDS - 1)], y_view(core, p), y_near.at[p & (SENDS - 1)])

    def near_remote(p):
        return pltpu.make_async_remote_copy(
            ybuf.at[p & (SENDS - 1)], y_view(core, p), y_near.at[p & (SENDS - 1)], ag_recv.at[core, lax.shift_right_logical(p, 1)], device_id={"sp": partner}, device_id_type=MESH)

    def far_remote(p):
        _, _, r = part(p)
        return pltpu.make_async_remote_copy(
            ybuf.at[p & (SENDS - 1)], y_view(core, p), y_far.at[p & (SENDS - 1)], ag_recv.at[core, lax.shift_right_logical(p, 1)],
            device_id={"tp": z_prev, "sp": 2 * row_y + r}, device_id_type=MESH)

    def wait_result_out(p):
        near_local(p).wait()
        far_remote(p).wait_send()

    def back_copy(owner, q):
        view = y_view(owner, 2 * q)
        z_to = jnp.clip(z - 1 + 2 * owner, 0, nz - 1)
        return pltpu.make_async_remote_copy(view, view, ag_send.at[owner, q], ag_recv.at[owner, q], device_id={"tp": z_to}, device_id_type=MESH)

    def sum_op(p):
        view = sum_view(p)

        @pl.when(hop > 0)
        def _():
            sum_copy(p).wait_recv()
            u, b, r = part(p)
            at = (u & 1, pl.ds(mult(r * rows, rows), rows), pl.ds(mult(b * bw, bw), bw))
            pbuf[at] = pbuf[at] + rbuf[p & (SLOTS - 1)]

            @pl.when(p + SLOTS < pieces)
            def _():
                pl.semaphore_signal(credit, inc=1, device_id={"tp": z_prev}, device_id_type=MESH)

        @pl.when(hop < nz - 1)
        def _():
            @pl.when(p >= SENDS)
            def _():
                sum_copy(p - SENDS).wait_send()

            @pl.when(p >= SLOTS)
            def _():
                pl.semaphore_wait(credit, 1)

            sum_copy(p).start()

        @pl.when(hop == nz - 1)
        def _():
            @pl.when(p >= SENDS)
            def _():
                wait_result_out(p - SENDS)

            slot = p & (SENDS - 1)
            pltpu.make_async_copy(x_own.at[pl.ds(0, rows), pl.ds(0, bw)], xbuf.at[slot], x_sem.at[slot]).wait()
            ybuf[slot] = (xbuf[slot].astype(F32) + view[...]).astype(BF16)

            @pl.when(p + 2 < pieces)
            def _():
                start_x(p + 2)

            far_remote(p).start()
            r = p & 1

            @pl.when(r == core)
            def _():
                near_local(p).start()

            @pl.when(r != core)
            def _():
                near_remote(p).start()

    def back_op(owner, q, distance):
        back_copy(owner, q).wait_recv()

        @pl.when((distance > 0) & (distance < nz - 1))
        def _():
            back_copy(owner, q).start()

    def ticks(t, count):
        def body(i, carry):
            tick(t + i)
            return carry

        lax.fori_loop(0, count, body, 0)

    shrink = math.gcd(per_unit, unit_ticks)
    rate = per_unit // shrink, unit_ticks // shrink

    def piece_at(v):
        v_ok = jnp.maximum(v, 0)
        p = over(rate[0] * v_ok + rate[1] - 1, rate[1])
        return p, (v >= 0) & (over(rate[1] * p, rate[0]) == v_ok) & (p < pieces)

    def tick(t):
        p, here = piece_at(t - 2 - hop * HOP)

        @pl.when(here)
        def _():
            sum_op(p)

        for owner in (0, 1):
            distance = nz - 1 - z if owner == 0 else z
            pb, back = piece_at(t - 3 - (nz - 1) * HOP - distance * BACK_HOP)
            mine = (distance == 0) & (core == owner)

            @pl.when(back & ((pb & 1) == core) & jnp.logical_not(mine))
            def _():
                back_op(owner, lax.shift_right_logical(pb, 1), distance)

    last_tick = (rate[1] * (pieces - 1)) // rate[0] + 3 + (nz - 1) * (HOP + BACK_HOP)

    def attend(u, r, s):
        first = u * rows + s * att
        token = (2 * row_y + r) * tokens + first
        q_rows = qbuf[r, pl.ds(mult(first, att), att), :]
        q_stack = jnp.concatenate([q_rows[:, i * HEAD_DIM:(i + 1) * HEAD_DIM] for i in range(heads)], axis=0)
        m_buf[...] = jnp.full_like(m_buf, -jnp.inf)
        l_buf[...] = jnp.zeros_like(l_buf)
        acc_buf[...] = jnp.zeros_like(acc_buf)

        def step(base, count, masked):
            starts = [mult(base + j * keys_step, keys_step) for j in range(count)]
            scores = []
            for start in starts:
                part = lax.dot_general(kbuf[pl.ds(start, keys_step), :], q_stack, (((1,), (1,)), ((), ())), preferred_element_type=F32)
                if masked:
                    key_id = start + lax.broadcasted_iota(jnp.int32, part.shape, 0)
                    token_id = token + (lax.broadcasted_iota(jnp.int32, part.shape, 1) & (att - 1))
                    part = jnp.where(key_id <= token_id, part, -jnp.inf)
                scores.append(part)
            m_old = m_buf[...]
            m_new = m_old
            for part in scores:
                m_new = jnp.maximum(m_new, jnp.max(part, axis=0, keepdims=True))
            m_buf[...] = m_new
            fade = jnp.exp2((m_old - m_new) * EXP2_SCALE)
            total, mixed = None, None
            for start, part in zip(starts, scores):
                w = jnp.exp2((part - m_new[0:1]) * EXP2_SCALE)
                w_sum = jnp.sum(w.reshape(keys_step // 8, 8, w.shape[1]), axis=0)
                w_v = jnp.dot(vtbuf[:, pl.ds(start, keys_step)], w.astype(BF16), preferred_element_type=F32)
                total = w_sum if total is None else total + w_sum
                mixed = w_v if mixed is None else mixed + w_v
            l_buf[...] = l_buf[...] * fade + total
            acc_buf[...] = acc_buf[...] * fade[0:1] + mixed

        span = 2 * keys_step
        spans = token // span

        def clear(i, carry):
            step(i * span, 2, False)
            return carry

        def edge(i, carry):
            step(spans * span + i * keys_step, 1, True)
            return carry

        lax.fori_loop(0, spans, clear, 0)
        lax.fori_loop(0, (token - spans * span) // keys_step + 1, edge, 0)
        out = (acc_buf[...] / jnp.sum(l_buf[...], axis=0, keepdims=True)).astype(BF16)
        for i in range(heads):
            abuf[u & 1, pl.ds(mult(r * rows + s * att, att), att), pl.ds(mult(core * q_cols + i * HEAD_DIM, HEAD_DIM), HEAD_DIM)] = out[:, i * att:(i + 1) * att].T

    start_gate_up(0)
    own_u_copy(0).start()
    start_gate_up(1)
    for copy in own_copies():
        copy.start()
    own_cache().start()

    @pl.when(hop == nz - 1)
    def _():
        start_x(0)
        start_x(1)

    barrier = pltpu.get_barrier_semaphore()
    for other in (partner, across, across_partner):
        pl.semaphore_signal(barrier, inc=1, device_id={"sp": other}, device_id_type=MESH)

    @pl.when(z > 0)
    def _():
        pl.semaphore_signal(barrier, inc=1, device_id={"tp": z - 1}, device_id_type=MESH)
        pl.semaphore_signal(barrier, inc=1, device_id={"tp": z - 1, "sp": partner}, device_id_type=MESH)

    @pl.when(z < nz - 1)
    def _():
        pl.semaphore_signal(barrier, inc=1, device_id={"tp": z + 1}, device_id_type=MESH)
        pl.semaphore_signal(barrier, inc=1, device_id={"tp": z + 1, "sp": partner}, device_id_type=MESH)

    pl.semaphore_wait(barrier, 3 + 2 * (z > 0).astype(jnp.int32) + 2 * (z < nz - 1).astype(jnp.int32))

    first_u_copy().start()
    for d in (1, 2, 0):
        for copy in key_copies(d):
            copy.start()
    q_copy().start()

    def send_u(u, carry):
        far_u_copy(u).start()
        return carry

    lax.fori_loop(1, units, send_u, 0)

    def unit(u, carry):
        t0 = u * unit_ticks
        gate_up_tick = t0 - 2 * nbg - 2 * subs
        own_u_copy(u).wait()

        @pl.when(u == 0)
        def _():
            first_u_copy().wait()

        @pl.when(u > 0)
        def _():
            par_u_copy(u).wait()

        for n in range(DOWN_SLOTS):
            down_copy(n).start()
        out_copy(0).start()
        out_copy(1).start()

        def gate_up(n, carry):
            slot = n & 1
            copy_g, copy_u = gate_up_copies(n)
            copy_g.wait()
            copy_u.wait()
            both = jnp.dot(ubuf[...], wgu_buf[slot], preferred_element_type=F32)
            hbuf[u & 1, :, pl.ds(mult(core * ff_half + n * bg, bg), bg)] = silu_mul(both[:, :bg], both[:, bg:])

            @pl.when(n + 2 < nbg)
            def _():
                start_gate_up(n + 2)

            ticks(gate_up_tick + 2 * n, 2)
            h_copy(u, n).start()
            return carry

        lax.fori_loop(0, nbg, gate_up, 0)

        @pl.when(u == 0)
        def _():
            for copy in own_copies():
                copy.wait()
            for d in range(3):
                for copy in key_copies(d):
                    copy.wait()
            q_copy().wait()
            for d in range(3):
                cache_copy(d).start()

        def sub(i, carry):
            r = over(i, subs)
            attend(u, r, i - r * subs)
            tick(t0 - 2 * subs + i)
            return carry

        lax.fori_loop(0, 2 * subs, sub, 0)
        a_copy(u).start()

        @pl.when(u + 1 < units)
        def _():
            own_u_copy(u + 1).start()
            far_u_copy(u + 1).wait()
            par_u_copy(u + 1).start()
            start_gate_up(0)
            start_gate_up(1)

        def wait_h(j, carry):
            h_copy(u, j).wait()
            return carry

        def down(b, carry):
            cols = pl.ds(mult(b * wb, wb), wb)
            own_rows = pl.ds(mult(core * ff_half, ff_half), ff_half)
            par_rows = pl.ds(mult((1 - core) * ff_half, ff_half), ff_half)
            down_copy(2 * b).wait()
            pbuf[u & 1, :, cols] = jnp.dot(hbuf[u & 1, :, own_rows], wd_buf[0], preferred_element_type=F32)

            @pl.when(b + 1 < nbw // 2)
            def _():
                down_copy(2 * b + 2).start()

            ticks(t0 + 4 * b, 2)

            @pl.when(b == 0)
            def _():
                lax.fori_loop(0, nbg, wait_h, 0)
                a_copy(u).wait()

            down_copy(2 * b + 1).wait()
            out_copy(b).wait()
            pbuf[u & 1, :, cols] = (
                pbuf[u & 1, :, cols]
                + jnp.dot(hbuf[u & 1, :, par_rows], wd_buf[1], preferred_element_type=F32)
                + jnp.dot(abuf[u & 1], wo_buf[b & 1], preferred_element_type=F32)
            )

            @pl.when(b + 1 < nbw // 2)
            def _():
                down_copy(2 * b + 3).start()

            @pl.when(b + 2 < nbw // 2)
            def _():
                out_copy(b + 2).start()

            ticks(t0 + 4 * b + 2, 2)
            return carry

        lax.fori_loop(0, nbw // 2, down, 0)
        return carry

    lax.fori_loop(0, units, unit, 0)

    def drain(t, carry):
        tick(t)
        return carry

    lax.fori_loop((units - 1) * unit_ticks + 2 * nbw, last_tick + 1, drain, 0)

    def sums_out(i, carry):
        p = pieces - SENDS + i

        @pl.when(hop < nz - 1)
        def _():
            sum_copy(p).wait_send()

        @pl.when(hop == nz - 1)
        def _():
            wait_result_out(p)

        return carry

    lax.fori_loop(0, SENDS, sums_out, 0)

    for owner in (0, 1):
        distance = nz - 1 - z if owner == 0 else z

        @pl.when((distance > 0) & (distance < nz - 1))
        def _():
            def backs_out(q, carry):
                back_copy(owner, q).wait_send()
                return carry

            lax.fori_loop(0, pieces // 2, backs_out, 0)

    own_cache().wait()
    for d in range(3):
        cache_copy(d).wait()


def layer(u_own, x_own, x_par, q_mine, q_other, kv, vt, w_gate, w_up, w_down, w_o):
    tokens, model = u_own.shape
    ff = w_gate.shape[1]
    ff_half, cols_half = ff // 2, model // 2
    rows = tokens // 4
    att = min(128, rows)
    bg, bw = block_of(ff_half, 256), block_of(cols_half, 512) // 2
    wb = 2 * bw
    nbg, nbw = ff_half // bg, cols_half // bw
    q_cols = q_mine.shape[1]
    kv_tokens = 4 * tokens
    keys_step = min(512, kv_tokens // 4)
    units = tokens // rows
    pieces = 2 * nbw * units
    stack = att * (q_cols // HEAD_DIM)
    any_spec = pl.BlockSpec(memory_space=pl.ANY)
    dma = pltpu.SemaphoreType.DMA
    macs = 2 * tokens * ff_half * model * 2 + 2 * tokens * ff * cols_half + 2 * tokens * w_o.shape[0] * cols_half
    y_out, cache, _ = pl.pallas_call(
        functools.partial(layer_kernel, rows, att, keys_step),
        out_shape=[
            jax.ShapeDtypeStruct((tokens, model), BF16),
            jax.ShapeDtypeStruct((kv_tokens, 2 * HEAD_DIM), BF16),
            jax.ShapeDtypeStruct((tokens, model), BF16),
        ],
        in_specs=[any_spec] * 11,
        out_specs=[any_spec] * 3,
        scratch_shapes=[
            pltpu.VMEM((2, model, 2 * bg), BF16),
            pltpu.VMEM((DOWN_SLOTS, ff_half, wb), BF16),
            pltpu.VMEM((2, w_o.shape[0], wb), BF16),
            pltpu.VMEM((2 * rows, model), BF16),
            pltpu.VMEM((2, 2 * rows, ff), BF16),
            pltpu.VMEM((2, 2 * rows, w_o.shape[0]), BF16),
            pltpu.VMEM((2, tokens, q_cols), BF16),
            pltpu.VMEM((kv_tokens, HEAD_DIM), BF16),
            pltpu.VMEM((HEAD_DIM, kv_tokens), BF16),
            pltpu.VMEM((2, 2 * rows, cols_half), F32),
            pltpu.VMEM((SLOTS, rows, bw), F32),
            pltpu.VMEM((SENDS, rows, bw), BF16),
            pltpu.VMEM((SENDS, rows, bw), BF16),
            pltpu.VMEM((8, stack), F32),
            pltpu.VMEM((8, stack), F32),
            pltpu.VMEM((HEAD_DIM, stack), F32),
            dma((2, 2)), dma((DOWN_SLOTS,)), dma((2,)), dma((2,)), dma((4,)), dma((units,)), dma((units,)), dma, dma, dma((3, 3)), dma((3, 3)),
            dma((nbg,)), dma((2, nbg)), dma, dma((2,)),
            dma((SENDS,)), dma((SLOTS,)), dma((SENDS,)), dma((SENDS,)), dma((SENDS,)),
            dma((2, pieces // 2)), dma((2, pieces // 2)),
            pltpu.SemaphoreType.REGULAR,
        ],
        compiler_params=pltpu.CompilerParams(
            collective_id=0, has_side_effects=True, vmem_limit_bytes=67043328),
        cost_estimate=pl.CostEstimate(flops=2 * macs, bytes_accessed=6 * ff_half * model * units, transcendentals=0),
        name="layer",
    )(u_own, x_own, x_par, q_mine, q_other, kv, vt, w_gate, w_up, w_down, w_o)
    return y_out, cache


def solution(mesh):
    row_spec = P(("rep", "sp"), None)
    cache_spec = P("rep", ("tp", "sp"), None)
    other_core = [(0, 1), (1, 0), (2, 3), (3, 2)]

    def layer_block(x_in, positions, norm_gain, w_q, w_k, w_v, w_o, w_gate, w_up, w_down):
        core = (lax.axis_index("sp") % 2).astype(jnp.int32).reshape(1)
        x_par = lax.ppermute(x_in, "sp", other_core)
        cos_tab, sin_tab = rope_tables(positions)
        normed, kv, vt, q_other, q_mine = project(core, x_in, norm_gain.reshape(1, -1), cos_tab, sin_tab, w_k, w_v, w_q)
        y_out, cache = layer(normed, x_in, x_par, q_mine, q_other, kv, vt, w_gate, w_up, w_down, w_o)
        return y_out, cache[:, None, :HEAD_DIM], cache[:, None, HEAD_DIM:]

    return jax.shard_map(
        layer_block,
        mesh=mesh,
        in_specs=(row_spec, P(("rep", "sp")), P(None), P(None, "tp"), P(None, "tp"), P(None, "tp"), P("tp", None), P(None, "tp"), P(None, "tp"), P("tp", None)),
        out_specs=(row_spec, cache_spec, cache_spec),
        check_vma=False,
    )
```

time: 675 us -> 582 us (0.86)
  Pallas kernels: 597 us -> 565 us
  matrix products: 29.3 us -> 0 us
  other arithmetic: 17.3 us -> 3.83 us
  local copies, waits for them, and re-layouts: 22 us -> 11.8 us
    pallas_call x2, Pallas kernels: 597 us -> 565 us  [the longest x1 524 us: layer(): pl.pallas_call(functools.partial(layer_kernel, rows, att, keys_step), out...]
    dot_general x3 -> x0, matrix products: 29.3 us -> none  [the longest x1 16.1 us: layer_block(): jnp.dot(normed, w_q, preferred_element_type=F32)]
  transfers between devices with their start and end apart: 6 -> 1, of which waited for: 0 -> 0; matrix products, arithmetic and copies ran while one was open for 8% -> 1% of each run, Pallas kernels for 89% -> 7%
where the time goes in v2:
time: 582 us
  Pallas kernels  565 us (97%)
  local copies, waits for them, and re-layouts  11.8 us (2%)
    pallas_call x1, Pallas kernels, layer(): pl.pallas_call(functools.partial(layer_kernel, rows, att, keys_step), out...  524 us
    pallas_call x1, Pallas kernels, project(): pl.pallas_call(qkv_kernel, grid_spec=pltpu.PrefetchScalarGridSpec(num_sca...  40.4 us
  transfers between devices with their start and end apart: 1, of which 0 were waited for; matrix products, arithmetic and copies ran while one was open for 1% of the time, Pallas kernels for 7%

profile of v2, /device:TPU:5, one launch (start us, length us, event | category | flops | bytes accessed | tf_op | source)
XLA Modules:
  0.0 581.9 jit_solution(12892836438892046220)
XLA Ops:
  0.6 0.7 collective-permute-start
  1.4 0.7 convert_element_type.3
  2.1 0.1 compare_select_fusion
  2.1 3.1 fusion
  5.2 40.4 %project.1 = (bf16[1024,5120]{1,0:T(8,128)(2,1)}, bf16[2,1024,256]{2,1,0:T(8,128)(2,1)}, bf16[2,128,1024]{2,1,0:T(8,128)(2,1)}, bf16[1024,512]{1,0:T(8,128)(2,1)}, bf16[1024,512]{1,0:T(8,128)(2,1)}) custom-call(s32[1]{0:T(128)} %bitcast.core_ref, bf16[1024,5120]{1,0:T(8,128)(2,1)} %x_own.1, f32[1,5120]{1,0:T(1,128)} %bitcast.6, ...), custom_call_target="tpu_custom_call" | custom-call | flops 16106127360 | bytes 31457280 | tf_op jit(solution)/shard_map/project/pallas_call | solution.py:101
  45.6 0.0 collective-permute-done.x_par
  45.6 524.5 %layer.1 = (bf16[1024,5120]{1,0:T(8,128)(2,1)}, bf16[4096,256]{1,0:T(8,128)(2,1)}, bf16[1024,5120]{1,0:T(8,128)(2,1)}) custom-call(bf16[1024,5120]{1,0:T(8,128)(2,1)} %get-tuple-element.10.u_own, bf16[1024,5120]{1,0:T(8,128)(2,1)} %x_own.1, bf16[1024,5120]{1,0:T(8,128)(2,1)} %collective-permute-done.x_par, bf16[1024,512]{1,0:T(8,128)(2,1)} %get-tuple-element.11.q_mine, ...), custom_call_target="tpu_custom_call" | custom-call | flops 268435456000 | bytes 503316480 | tf_op jit(solution)/shard_map/layer/pallas_call | solution.py:654
  570.1 3.0 slice_bitcast_fusion
  573.1 8.8 %copy.14 = bf16[1024,5120]{1,0:T(8,128)(2,1)} copy(bf16[1024,5120]{1,0:T(8,128)(2,1)} %get-tuple-element.26) | data formatting | bytes 20971520
  (1 shorter events, 0.0 us)
Async XLA Ops:
  0.6 45.0 %collective-permute-start = (bf16[1024,5120]{1,0:T(8,128)(2,1)}, bf16[1024,5120]{1,0:T(8,128)(2,1)}, u32[]{:S(2)}, u32[]{:S(2)}) collective-permute-start(bf16[1024,5120]{1,0:T(8,128)(2,1)} %x_own.1), channel_id=1, source_target_pairs={{0,1},{1,0},{2,3},{3,2},{4,5},{5,4},{6,7},{7,6},{8,9},{9,8},{10,11... | collective-permute-start | bytes 31457288 | tf_op jit(solution)/shard_map/ppermute | solution.py:701

commit v3 on v2

v3 whole, which is shorter than its diff:
```python
import functools

import jax
import jax.numpy as jnp
from jax import lax
from jax.experimental import pallas as pl
from jax.experimental.pallas import tpu as pltpu
from jax.sharding import PartitionSpec as P

HEAD_DIM = 128
EPS = 1e-6
ROPE_BASE = 500000.0
EXP2_SCALE = HEAD_DIM ** -0.5 * 1.4426950408889634
MESH = pl.DeviceIdType.MESH
F32 = jnp.float32
BF16 = jnp.bfloat16

SLOTS = 4
SENDS = 4
HOP = 6
BACK_HOP = 8
DOWN_SLOTS = 2
RATE = 5, 13


def block_of(size, most):
    return most if size % most == 0 else most // 2


def odd(x):
    return x & 1


def below(n):
    return n - 1


def over(x, d):
    if d & (d - 1) == 0:
        return lax.shift_right_logical(x, d.bit_length() - 1)
    return lax.shift_right_logical(x * (65536 // d + 1), 16)


def rope_tables(positions):
    inv_freq = ROPE_BASE ** (-(jnp.arange(HEAD_DIM // 2, dtype=F32) * (2.0 / HEAD_DIM)))
    angles = positions.astype(F32)[:, None] * jnp.concatenate([inv_freq, inv_freq])[None, :]
    sign = jnp.where(jnp.arange(HEAD_DIM) < HEAD_DIM // 2, -1.0, 1.0)
    return jnp.cos(angles), jnp.sin(angles) * sign[None, :]


def rotate(vectors, cos_tab, sin_tab):
    return (vectors * cos_tab + pltpu.roll(vectors, HEAD_DIM // 2, 1) * sin_tab).astype(BF16)


def silu_mul(gate, up):
    return (gate / (1.0 + jnp.exp(-gate)) * up).astype(BF16)


def qkv_kernel(core_ref, x_ref, gain_ref, cos_ref, sin_ref, wk_ref, wv_ref, wq_ref, u_ref, kv_ref, vt_ref, q_other_ref, q_mine_ref, u_buf, inv_buf, wq_buf, wq_sem):
    phase, block = pl.program_id(0), pl.program_id(1)
    rows = x_ref.shape[0]
    at = pl.ds(pl.multiple_of(block * rows, rows), rows)
    q_cols = wq_buf.shape[2]
    core = core_ref[0]

    def weights(i):
        group = jnp.where(i == 0, 1 - core, core)
        return pltpu.make_async_copy(wq_ref.at[:, pl.ds(pl.multiple_of(group * q_cols, q_cols), q_cols)], wq_buf.at[i], wq_sem.at[i])

    @pl.when((phase == 0) & (block == 0))
    def _():
        weights(0).start()
        weights(1).start()

    @pl.when(phase == 0)
    def _():
        step = 16
        model = x_ref.shape[1]

        def squares(i, carry):
            part = pl.ds(pl.multiple_of(i * step, step), step)
            total = jnp.zeros((step, 128), F32)
            for j in range(model // 128):
                x = x_ref[part, j * 128:(j + 1) * 128].astype(F32)
                total = total + x * x
            inv_buf[part, :] = total
            return carry

        lax.fori_loop(0, rows // step, squares, 0, unroll=2)
        mean = jnp.sum(inv_buf[...], axis=1, keepdims=True) * (1.0 / model)
        inv_buf[...] = jnp.broadcast_to(lax.rsqrt(mean + EPS), inv_buf.shape)

        def scale(i, carry):
            part = pl.ds(pl.multiple_of(i * step, step), step)
            inv = inv_buf[part, :]
            for j in range(model // 128):
                cols = slice(j * 128, (j + 1) * 128)
                u = (x_ref[part, cols].astype(F32) * inv * gain_ref[:, cols]).astype(BF16)
                u_ref[part, cols] = u
                u_buf[pl.ds(pl.multiple_of(block * rows + i * step, step), step), cols] = u
            return carry

        lax.fori_loop(0, rows // step, scale, 0, unroll=2)
        k = jnp.dot(u_ref[...], wk_ref[...], preferred_element_type=F32)
        v = jnp.dot(u_ref[...], wv_ref[...], preferred_element_type=F32)
        for head in range(2):
            cols = slice(head * HEAD_DIM, (head + 1) * HEAD_DIM)
            kv_ref[head, :, :HEAD_DIM] = rotate(k[:, cols], cos_ref[at, :], sin_ref[at, :])
            kv_ref[head, :, HEAD_DIM:] = v[:, cols].astype(BF16)
            vt_ref[head] = v[:, cols].T.astype(BF16)

    def queries(q_ref, i):
        pl.when(block == 0)(lambda: weights(i).wait())
        q = jnp.dot(u_buf[at, :], wq_buf[i], preferred_element_type=F32)
        for head in range(q.shape[1] // HEAD_DIM):
            cols = slice(head * HEAD_DIM, (head + 1) * HEAD_DIM)
            q_ref[:, cols] = rotate(q[:, cols], cos_ref[at, :], sin_ref[at, :])

    pl.when(phase == 1)(lambda: queries(q_other_ref, 0))
    pl.when(phase == 2)(lambda: queries(q_mine_ref, 1))


def project(core, x_in, gain, cos_tab, sin_tab, w_k, w_v, w_q):
    tokens, model = x_in.shape
    rows = min(256, tokens // 2)
    blocks = tokens // rows
    q_cols = w_q.shape[1] // 2
    last = blocks - 1

    def first(p, i):
        return jnp.where(p == 0, i, last)

    return pl.pallas_call(
        qkv_kernel,
        grid_spec=pltpu.PrefetchScalarGridSpec(
            num_scalar_prefetch=1,
            grid=(3, blocks),
            in_specs=[
                pl.BlockSpec((rows, model), lambda p, i, c: (first(p, i), 0)),
                pl.BlockSpec((1, model), lambda p, i, c: (0, 0)),
                pl.BlockSpec((tokens, HEAD_DIM), lambda p, i, c: (0, 0)),
                pl.BlockSpec((tokens, HEAD_DIM), lambda p, i, c: (0, 0)),
                pl.BlockSpec((model, 2 * HEAD_DIM), lambda p, i, c: (0, 0)),
                pl.BlockSpec((model, 2 * HEAD_DIM), lambda p, i, c: (0, 0)),
                pl.BlockSpec(memory_space=pl.ANY),
            ],
            out_specs=[
                pl.BlockSpec((rows, model), lambda p, i, c: (first(p, i), 0)),
                pl.BlockSpec((2, rows, 2 * HEAD_DIM), lambda p, i, c: (0, first(p, i), 0)),
                pl.BlockSpec((2, HEAD_DIM, rows), lambda p, i, c: (0, 0, first(p, i))),
                pl.BlockSpec((rows, q_cols), lambda p, i, c: (jnp.where(p == 0, 0, jnp.where(p == 1, i, last)), 0)),
                pl.BlockSpec((rows, q_cols), lambda p, i, c: (jnp.where(p == 2, i, 0), 0)),
            ],
            scratch_shapes=[pltpu.VMEM((tokens, model), BF16), pltpu.VMEM((rows, 128), F32), pltpu.VMEM((2, model, q_cols), BF16), pltpu.SemaphoreType.DMA((2,))],
        ),
        out_shape=[
            jax.ShapeDtypeStruct((tokens, model), BF16),
            jax.ShapeDtypeStruct((2, tokens, 2 * HEAD_DIM), BF16),
            jax.ShapeDtypeStruct((2, HEAD_DIM, tokens), BF16),
            jax.ShapeDtypeStruct((tokens, q_cols), BF16),
            jax.ShapeDtypeStruct((tokens, q_cols), BF16),
        ],
        compiler_params=pltpu.CompilerParams(vmem_limit_bytes=60 * 2 ** 20),
        cost_estimate=pl.CostEstimate(flops=2 * tokens * model * (2 * q_cols + 4 * HEAD_DIM), bytes_accessed=6 * tokens * model, transcendentals=0),
        name="project",
    )(core, x_in, gain, cos_tab, sin_tab, w_k, w_v, w_q)


def layer_kernel(
    rows, att, keys_step,
    u_own, x_own, x_par, gain_ref, q_mine, q_other, kv, vt, w_gate, w_up, w_down, w_o,
    y_out, cache, u_par,
    wgu_buf, wd_buf, wo_buf, ubuf, hbuf, abuf, qbuf, kbuf, vtbuf, pbuf, rbuf, xbuf, ybuf, m_buf, l_buf, acc_buf, s0_buf, s1_buf, top_buf,
    wgu_sem, wd_sem, wo_sem, u_sem, near_sem, u_send, u_recv, q_send, q_recv, kv_send, kv_recv,
    h_send, h_recv, a_send, a_recv, lend_send, lend_recv, rs_send, rs_recv, x_sem, y_near, y_far, ag_recv, ag_send, credit,
):
    tokens, model = u_own.shape
    units = tokens // rows
    ff_half = w_gate.shape[1] // 2
    cols_half = model // 2
    bg = wgu_buf.shape[2] // 2
    wb = wd_buf.shape[2]
    bw = wb // 2
    nbg = ff_half // bg
    nbw = cols_half // bw
    q_cols = q_mine.shape[1]
    heads = q_cols // HEAD_DIM
    subs = rows // att
    per_unit = 2 * nbw
    pieces = per_unit * units
    unit_ticks = 2 * nbg + 2 * subs + 2 * nbw
    lent = below(units)

    z = lax.axis_index("tp")
    nz = lax.axis_size("tp")
    end = below(nz)
    sp = lax.axis_index("sp")
    core = sp % 2
    row_y = sp // 2
    twin = 1 - core
    partner = sp + twin - core
    other_y = 1 - row_y
    across = 2 * other_y + core
    across_partner = 2 * other_y + twin
    step_z = 1 - 2 * core
    hop = jnp.where(core == 0, z, end - z)
    z_next = jnp.clip(z + step_z, 0, end)
    z_prev = jnp.clip(z - step_z, 0, end)

    def mult(value, of):
        return pl.multiple_of(value, of)

    def gate_up_copies(n):
        cols = pl.ds(mult(core * ff_half + n * bg, bg), bg)
        slot = odd(n)
        return (
            pltpu.make_async_copy(w_gate.at[:, cols], wgu_buf.at[slot, :, pl.ds(0, bg)], wgu_sem.at[slot, 0]),
            pltpu.make_async_copy(w_up.at[:, cols], wgu_buf.at[slot, :, pl.ds(bg, bg)], wgu_sem.at[slot, 1]),
        )

    def start_gate_up(n):
        for copy in gate_up_copies(n):
            copy.start()

    def down_copy(n):
        b, k = n // 2, n % 2
        half = jnp.where(k == 0, core, twin)
        src = w_down.at[pl.ds(mult(half * ff_half, ff_half), ff_half), pl.ds(mult(core * cols_half + b * wb, wb), wb)]
        slot = n % DOWN_SLOTS
        return pltpu.make_async_copy(src, wd_buf.at[slot], wd_sem.at[slot])

    def out_copy(b):
        return pltpu.make_async_copy(w_o.at[:, pl.ds(mult(core * cols_half + b * wb, wb), wb)], wo_buf.at[odd(b)], wo_sem.at[odd(b)])

    def u_rows(u):
        return pl.ds(mult(u * rows, rows), rows)

    def own_u_copy(u):
        return pltpu.make_async_copy(u_own.at[u_rows(u), :], ubuf.at[u_rows(core), :], u_sem.at[0])

    def par_u_copy(u):
        return pltpu.make_async_copy(u_par.at[u_rows(u), :], ubuf.at[u_rows(twin), :], u_sem.at[1])

    def par_x_copy():
        return pltpu.make_async_copy(x_par.at[u_rows(0), :], ubuf.at[u_rows(twin), :], u_sem.at[1])

    def norm_par_rows():
        step = 16

        def body(i, carry):
            at = pl.ds(mult((twin) * rows + i * step, step), step)
            total = jnp.zeros((step, 128), F32)
            for j in range(model // 128):
                x = ubuf[at, j * 128:(j + 1) * 128].astype(F32)
                total = total + x * x
            inv = lax.rsqrt(jnp.sum(total, axis=1, keepdims=True) * (1.0 / model) + EPS)
            for j in range(model // 128):
                cols = slice(j * 128, (j + 1) * 128)
                ubuf[at, cols] = (ubuf[at, cols].astype(F32) * inv * gain_ref[:, cols]).astype(BF16)
            return carry

        lax.fori_loop(0, rows // step, body, 0, unroll=2 if rows % (2 * step) == 0 else 1)

    all_tokens = pl.ds(0, tokens)

    own_tokens = pl.ds(mult(sp * tokens, tokens), tokens)

    def own_copies():
        return (
            pltpu.make_async_copy(q_mine, qbuf.at[core, all_tokens, :], near_sem.at[0]),
            pltpu.make_async_copy(kv.at[core, :, pl.ds(0, HEAD_DIM)], kbuf.at[own_tokens, :], near_sem.at[1]),
            pltpu.make_async_copy(vt.at[core], vtbuf.at[:, own_tokens], near_sem.at[2]),
        )

    def own_cache():
        return pltpu.make_async_copy(kv.at[row_y], cache.at[own_tokens, :], near_sem.at[3])

    def h_copy(u, j):
        view = hbuf.at[odd(u), :, pl.ds(mult(core * ff_half + j * bg, bg), bg)]
        return pltpu.make_async_remote_copy(view, view, h_send.at[j], h_recv.at[odd(u), j], device_id={"sp": partner}, device_id_type=MESH)

    def far_u_copy(u):
        return pltpu.make_async_remote_copy(
            u_own.at[u_rows(u), :], u_par.at[u_rows(u), :], u_send.at[u], u_recv.at[u], device_id={"sp": partner}, device_id_type=MESH)

    def q_copy():
        return pltpu.make_async_remote_copy(q_other, qbuf.at[core, all_tokens, :], q_send, q_recv, device_id={"sp": partner}, device_id_type=MESH)

    peers = ((partner, twin, row_y), (across, core, other_y), (across_partner, twin, other_y))

    def key_copies(d):
        to, head, _ = peers[d]
        return (
            pltpu.make_async_remote_copy(
                kv.at[head, :, pl.ds(0, HEAD_DIM)], kbuf.at[own_tokens, :], kv_send.at[0, d], kv_recv.at[0, d], device_id={"sp": to}, device_id_type=MESH),
            pltpu.make_async_remote_copy(
                vt.at[head], vtbuf.at[:, own_tokens], kv_send.at[1, d], kv_recv.at[1, d], device_id={"sp": to}, device_id_type=MESH),
        )

    def cache_copy(d):
        to, _, head = peers[d]
        return pltpu.make_async_remote_copy(
            kv.at[head], cache.at[own_tokens, :], kv_send.at[2, d], kv_recv.at[2, d], device_id={"sp": to}, device_id_type=MESH)

    def a_copy(u):
        view = abuf.at[odd(u), :, pl.ds(mult(core * q_cols, q_cols), q_cols)]
        return pltpu.make_async_remote_copy(view, view, a_send, a_recv.at[odd(u)], device_id={"sp": partner}, device_id_type=MESH)

    def lend_copies():
        rows_there = pl.ds(tokens, rows)
        return tuple(
            pltpu.make_async_remote_copy(
                src.at[u_rows(lent), :], qbuf.at[core, rows_there, :], lend_send.at[0, d], lend_recv.at[0, d], device_id={"sp": to}, device_id_type=MESH)
            for d, (src, to) in enumerate(((q_mine, across), (q_other, across_partner)))
        )

    def lent_copies():
        view = abuf.at[2, :, pl.ds(mult(core * q_cols, q_cols), q_cols)]
        return tuple(
            pltpu.make_async_remote_copy(view, view, lend_send.at[1, d], lend_recv.at[1, d], device_id={"sp": to}, device_id_type=MESH)
            for d, to in enumerate((across, across_partner))
        )

    def part(p):
        u = over(p, per_unit)
        i = p - u * per_unit
        return u, lax.shift_right_logical(i, 1), odd(i)

    def sum_view(p):
        u, b, r = part(p)
        return pbuf.at[odd(u), pl.ds(mult(r * rows, rows), rows), pl.ds(mult(b * bw, bw), bw)]

    def sum_copy(p):
        return pltpu.make_async_remote_copy(
            sum_view(p), rbuf.at[p & (SLOTS - 1)], rs_send.at[p & (SENDS - 1)], rs_recv.at[p & (SLOTS - 1)], device_id={"tp": z_next}, device_id_type=MESH)

    def y_view(owner, p):
        u, b, _ = part(p)
        return y_out.at[pl.ds(mult(u * rows, rows), rows), pl.ds(mult(owner * cols_half + b * bw, bw), bw)]

    def start_x(p):
        u, b, r = part(p)
        src = (pl.ds(mult(u * rows, rows), rows), pl.ds(mult(core * cols_half + b * bw, bw), bw))

        @pl.when(r == core)
        def _():
            pltpu.make_async_copy(x_own.at[src[0], src[1]], xbuf.at[odd(p)], x_sem.at[odd(p)]).start()

        @pl.when(r != core)
        def _():
            pltpu.make_async_copy(x_par.at[src[0], src[1]], xbuf.at[odd(p)], x_sem.at[odd(p)]).start()

    def near_local(p):
        return pltpu.make_async_copy(ybuf.at[p & (SENDS - 1)], y_view(core, p), y_near.at[p & (SENDS - 1)])

    def near_remote(p):
        return pltpu.make_async_remote_copy(
            ybuf.at[p & (SENDS - 1)], y_view(core, p), y_near.at[p & (SENDS - 1)], ag_recv.at[core, lax.shift_right_logical(p, 1)], device_id={"sp": partner}, device_id_type=MESH)

    def far_remote(p):
        _, _, r = part(p)
        return pltpu.make_async_remote_copy(
            ybuf.at[p & (SENDS - 1)], y_view(core, p), y_far.at[p & (SENDS - 1)], ag_recv.at[core, lax.shift_right_logical(p, 1)],
            device_id={"tp": z_prev, "sp": 2 * row_y + r}, device_id_type=MESH)

    def wait_result_out(p):
        near_local(p).wait()
        far_remote(p).wait_send()

    def back_copy(owner, q):
        view = y_view(owner, 2 * q)
        z_to = jnp.clip(z - 1 + 2 * owner, 0, end)
        return pltpu.make_async_remote_copy(view, view, ag_send.at[owner, q], ag_recv.at[owner, q], device_id={"tp": z_to}, device_id_type=MESH)

    def sum_op(p):
        view = sum_view(p)

        @pl.when(hop > 0)
        def _():
            sum_copy(p).wait_recv()
            u, b, r = part(p)
            at = (odd(u), pl.ds(mult(r * rows, rows), rows), pl.ds(mult(b * bw, bw), bw))
            pbuf[at] = pbuf[at] + rbuf[p & (SLOTS - 1)]

            @pl.when(p + SLOTS < pieces)
            def _():
                pl.semaphore_signal(credit, inc=1, device_id={"tp": z_prev}, device_id_type=MESH)

        @pl.when(hop < end)
        def _():
            @pl.when(p >= SENDS)
            def _():
                sum_copy(p - SENDS).wait_send()

            @pl.when(p >= SLOTS)
            def _():
                pl.semaphore_wait(credit, 1)

            sum_copy(p).start()

        @pl.when(hop == end)
        def _():
            @pl.when(p >= SENDS)
            def _():
                wait_result_out(p - SENDS)

            slot = p & (SENDS - 1)
            pltpu.make_async_copy(x_own.at[pl.ds(0, rows), pl.ds(0, bw)], xbuf.at[odd(p)], x_sem.at[odd(p)]).wait()
            ybuf[slot] = (xbuf[odd(p)].astype(F32) + view[...]).astype(BF16)

            @pl.when(p + 2 < pieces)
            def _():
                start_x(p + 2)

            far_remote(p).start()
            r = odd(p)

            @pl.when(r == core)
            def _():
                near_local(p).start()

            @pl.when(r != core)
            def _():
                near_remote(p).start()

    def back_op(owner, q, distance):
        back_copy(owner, q).wait_recv()

        @pl.when((distance > 0) & (distance < end))
        def _():
            back_copy(owner, q).start()

    def ticks(t, count):
        def body(i, carry):
            tick(t + i)
            return carry

        lax.fori_loop(0, count, body, 0)

    many, span_of = RATE

    def piece_at(v, span, per):
        v_ok = jnp.maximum(v, 0)
        u = over(v_ok, span)
        w = v_ok - u * span
        i = over(many * w + span_of - 1, span_of)
        return u * per + i, (v >= 0) & (span_of * i - many * w < many) & (i < per) & (u < units)

    first_back = 7 + end * HOP

    def tick(t):
        p, here = piece_at(t - 3 - hop * HOP, unit_ticks, per_unit)

        @pl.when(here)
        def _():
            sum_op(p)

        owner = odd(t)
        distance = jnp.where(owner == 0, end - z, z)
        q, back = piece_at(lax.shift_right_arithmetic(t - first_back - distance * BACK_HOP, 1), unit_ticks // 2, nbw)

        @pl.when(back & ((distance > 0) | (core != owner)))
        def _():
            back_op(owner, q, distance)

    last_tick = below(units) * unit_ticks + 2 * (span_of * nbw // many + 1) + first_back + end * BACK_HOP + 2

    def attend(first, token, slot, r, s):
        q_rows = qbuf[r, pl.ds(mult(first, att), att), :]
        q_stack = jnp.concatenate([q_rows[:, i * HEAD_DIM:(i + 1) * HEAD_DIM] for i in range(heads)], axis=0)
        m_buf[...] = jnp.full_like(m_buf, -jnp.inf)
        l_buf[...] = jnp.zeros_like(l_buf)
        acc_buf[...] = jnp.zeros_like(acc_buf)

        def stage(held, held_start, fresh, fresh_start, masked=False):
            if fresh is not None:
                start = mult(fresh_start, keys_step)
                part = lax.dot_general(kbuf[pl.ds(start, keys_step), :], q_stack, (((1,), (1,)), ((), ())), preferred_element_type=F32)
                if masked:
                    key_id = start + lax.broadcasted_iota(jnp.int32, part.shape, 0)
                    token_id = token + (lax.broadcasted_iota(jnp.int32, part.shape, 1) & (att - 1))
                    part = jnp.where(key_id <= token_id, part, -jnp.inf)
                fresh[...] = part
                top = jnp.max(part.reshape(keys_step // 8, 8, part.shape[1]), axis=0)
            if held is not None:
                m_old = m_buf[...]
                m_new = jnp.maximum(m_old, jnp.max(top_buf[...], axis=0, keepdims=True))
                m_buf[...] = m_new
                fade = jnp.exp2((m_old - m_new) * EXP2_SCALE)
                w = jnp.exp2((held[...] - m_new[0:1]) * EXP2_SCALE)
                l_buf[...] = l_buf[...] * fade + jnp.sum(w.reshape(keys_step // 8, 8, w.shape[1]), axis=0)
                acc_buf[...] = acc_buf[...] * fade[0:1] + jnp.dot(
                    vtbuf[:, pl.ds(mult(held_start, keys_step), keys_step)], w.astype(BF16), preferred_element_type=F32)
            if fresh is not None:
                top_buf[...] = top

        clear = token // keys_step
        edge = clear * keys_step
        stage(None, None, s0_buf, edge, True)

        def pair(i, carry):
            stage(s0_buf, jnp.where(i == 0, edge, (2 * i - 1) * keys_step), s1_buf, 2 * i * keys_step)
            stage(s1_buf, 2 * i * keys_step, s0_buf, (2 * i + 1) * keys_step)
            return carry

        pairs = clear // 2
        lax.fori_loop(0, pairs, pair, 0)
        held = jnp.where(pairs == 0, edge, (2 * pairs - 1) * keys_step)

        @pl.when(clear % 2 == 1)
        def _():
            stage(s0_buf, held, s1_buf, (clear - 1) * keys_step)
            stage(s1_buf, (clear - 1) * keys_step, None, None)

        @pl.when(clear % 2 == 0)
        def _():
            stage(s0_buf, held, None, None)

        out = (acc_buf[...] / jnp.sum(l_buf[...], axis=0, keepdims=True)).astype(BF16)
        for i in range(heads):
            abuf[slot, pl.ds(mult(r * rows + s * att, att), att), pl.ds(mult(core * q_cols + i * HEAD_DIM, HEAD_DIM), HEAD_DIM)] = out[:, i * att:(i + 1) * att].T

    start_gate_up(0)
    par_x_copy().start()
    own_u_copy(0).start()
    start_gate_up(1)
    for copy in own_copies():
        copy.start()
    own_cache().start()

    @pl.when(hop == end)
    def _():
        start_x(0)
        start_x(1)

    barrier = pltpu.get_barrier_semaphore()
    for other in (partner, across, across_partner):
        pl.semaphore_signal(barrier, inc=1, device_id={"sp": other}, device_id_type=MESH)

    @pl.when(z > 0)
    def _():
        pl.semaphore_signal(barrier, inc=1, device_id={"tp": z - 1}, device_id_type=MESH)
        pl.semaphore_signal(barrier, inc=1, device_id={"tp": z - 1, "sp": partner}, device_id_type=MESH)

    @pl.when(z < end)
    def _():
        pl.semaphore_signal(barrier, inc=1, device_id={"tp": z + 1}, device_id_type=MESH)
        pl.semaphore_signal(barrier, inc=1, device_id={"tp": z + 1, "sp": partner}, device_id_type=MESH)

    par_x_copy().wait()
    norm_par_rows()
    pl.semaphore_wait(barrier, 3 + 2 * (z > 0).astype(jnp.int32) + 2 * (z < end).astype(jnp.int32))

    for d in (1, 2, 0):
        for copy in key_copies(d):
            copy.start()
    q_copy().start()

    @pl.when(row_y == 1)
    def _():
        for copy in lend_copies():
            copy.start()

    def send_u(u, carry):
        far_u_copy(u).start()
        return carry

    lax.fori_loop(1, units, send_u, 0)

    def unit(u, carry):
        t0 = u * unit_ticks
        gate_up_tick = t0 - 2 * nbg - 2 * subs
        own_u_copy(u).wait()

        @pl.when(u > 0)
        def _():
            par_u_copy(u).wait()

        for n in range(DOWN_SLOTS):
            down_copy(n).start()
        out_copy(0).start()
        out_copy(1).start()

        def gate_up(n, carry):
            slot = odd(n)
            copy_g, copy_u = gate_up_copies(n)
            copy_g.wait()
            copy_u.wait()
            both = jnp.dot(ubuf[...], wgu_buf[slot], preferred_element_type=F32)
            hbuf[odd(u), :, pl.ds(mult(core * ff_half + n * bg, bg), bg)] = silu_mul(both[:, :bg], both[:, bg:])

            @pl.when(n + 2 < nbg)
            def _():
                start_gate_up(n + 2)

            ticks(gate_up_tick + 2 * n, 2)
            h_copy(u, n).start()
            return carry

        lax.fori_loop(0, nbg, gate_up, 0)

        @pl.when(u == 0)
        def _():
            for copy in own_copies():
                copy.wait()
            for d in range(3):
                for copy in key_copies(d):
                    copy.wait()
            q_copy().wait()
            for d in range(3):
                cache_copy(d).start()

        borrows = (row_y == 0) & (u == lent - 1)
        lends = (row_y == 1) & (u == lent)
        a_slot = jnp.where(lends, 2, odd(u))

        @pl.when(borrows)
        def _():
            for copy in lend_copies():
                copy.wait_recv()

        def sub(i, carry):
            mine = i < 2 * subs
            j = jnp.where(mine, i, i - 2 * subs)
            r = over(j, subs)
            part = j - r * subs
            first = jnp.where(mine, u * rows, tokens) + part * att
            token = jnp.where(mine, (2 * row_y + r) * tokens + u * rows, (2 + r) * tokens + lent * rows) + part * att
            attend(first, token, jnp.where(mine, odd(u), 2), r, part)
            ticks(t0 - 2 * subs + i, mine.astype(jnp.int32))
            return carry

        lax.fori_loop(0, jnp.where(lends, 0, jnp.where(borrows, 4 * subs, 2 * subs)), sub, 0)

        @pl.when(lends)
        def _():
            ticks(t0 - 2 * subs, 2 * subs)

        @pl.when(jnp.logical_not(lends))
        def _():
            a_copy(u).start()

        @pl.when(borrows)
        def _():
            for copy in lent_copies():
                copy.start()

        @pl.when(u + 1 < units)
        def _():
            own_u_copy(u + 1).start()
            far_u_copy(u + 1).wait()
            par_u_copy(u + 1).start()
            start_gate_up(0)
            start_gate_up(1)

        def wait_h(j, carry):
            h_copy(u, j).wait()
            return carry

        def down(b, carry):
            cols = pl.ds(mult(b * wb, wb), wb)
            own_rows = pl.ds(mult(core * ff_half, ff_half), ff_half)
            par_rows = pl.ds(mult((twin) * ff_half, ff_half), ff_half)
            down_copy(2 * b).wait()
            pbuf[odd(u), :, cols] = jnp.dot(hbuf[odd(u), :, own_rows], wd_buf[0], preferred_element_type=F32)

            @pl.when(b + 1 < nbw // 2)
            def _():
                down_copy(2 * b + 2).start()

            ticks(t0 + 4 * b, 2)

            @pl.when(b == 0)
            def _():
                lax.fori_loop(0, nbg, wait_h, 0)

                @pl.when(lends)
                def _():
                    for copy in lent_copies():
                        copy.wait_recv()

                @pl.when(jnp.logical_not(lends))
                def _():
                    a_copy(u).wait()

            down_copy(2 * b + 1).wait()
            out_copy(b).wait()
            pbuf[odd(u), :, cols] = (
                pbuf[odd(u), :, cols]
                + jnp.dot(hbuf[odd(u), :, par_rows], wd_buf[1], preferred_element_type=F32)
                + jnp.dot(abuf[a_slot], wo_buf[odd(b)], preferred_element_type=F32)
            )

            @pl.when(b + 1 < nbw // 2)
            def _():
                down_copy(2 * b + 3).start()

            @pl.when(b + 2 < nbw // 2)
            def _():
                out_copy(b + 2).start()

            ticks(t0 + 4 * b + 2, 2)
            return carry

        lax.fori_loop(0, nbw // 2, down, 0)
        return carry

    lax.fori_loop(0, units, unit, 0)

    def drain(t, carry):
        tick(t)
        return carry

    lax.fori_loop(below(units) * unit_ticks + 2 * nbw, last_tick + 1, drain, 0)

    def sums_out(i, carry):
        p = pieces - SENDS + i

        @pl.when(hop < end)
        def _():
            sum_copy(p).wait_send()

        @pl.when(hop == end)
        def _():
            wait_result_out(p)

        return carry

    lax.fori_loop(0, SENDS, sums_out, 0)

    for owner in (0, 1):
        distance = end - z if owner == 0 else z

        @pl.when((distance > 0) & (distance < end))
        def _():
            def backs_out(q, carry):
                back_copy(owner, q).wait_send()
                return carry

            lax.fori_loop(0, pieces // 2, backs_out, 0)

    own_cache().wait()
    for d in range(3):
        cache_copy(d).wait()

    @pl.when(row_y == 1)
    def _():
        for copy in lend_copies():
            copy.wait_send()

    @pl.when(row_y == 0)
    def _():
        for copy in lent_copies():
            copy.wait_send()


def layer(u_own, x_own, x_par, gain, q_mine, q_other, kv, vt, w_gate, w_up, w_down, w_o):
    tokens, model = u_own.shape
    ff = w_gate.shape[1]
    ff_half, cols_half = ff // 2, model // 2
    rows = tokens // 4
    att = min(128, rows)
    bg, bw = block_of(ff_half, 256), block_of(cols_half, 512) // 2
    wb = 2 * bw
    nbg, nbw = ff_half // bg, cols_half // bw
    q_cols = q_mine.shape[1]
    kv_tokens = 4 * tokens
    keys_step = min(512, kv_tokens // 4)
    units = tokens // rows
    pieces = 2 * nbw * units
    stack = att * (q_cols // HEAD_DIM)
    any_spec = pl.BlockSpec(memory_space=pl.ANY)
    dma = pltpu.SemaphoreType.DMA
    two, sends, quad, peer = dma((2,)), dma((SENDS,)), dma((2, 2)), dma((3, 3))
    macs = tokens * model * (3 * ff + w_o.shape[0])
    y_out, cache, _ = pl.pallas_call(
        functools.partial(layer_kernel, rows, att, keys_step),
        out_shape=[
            jax.ShapeDtypeStruct((tokens, model), BF16),
            jax.ShapeDtypeStruct((kv_tokens, 2 * HEAD_DIM), BF16),
            jax.ShapeDtypeStruct((tokens, model), BF16),
        ],
        in_specs=[any_spec] * 3 + [pl.BlockSpec(memory_space=pltpu.VMEM)] + [any_spec] * 8,
        out_specs=[any_spec] * 3,
        scratch_shapes=[
            pltpu.VMEM((2, model, 2 * bg), BF16),
            pltpu.VMEM((DOWN_SLOTS, ff_half, wb), BF16),
            pltpu.VMEM((2, w_o.shape[0], wb), BF16),
            pltpu.VMEM((2 * rows, model), BF16),
            pltpu.VMEM((2, 2 * rows, ff), BF16),
            pltpu.VMEM((3, 2 * rows, w_o.shape[0]), BF16),
            pltpu.VMEM((2, tokens + rows, q_cols), BF16),
            pltpu.VMEM((kv_tokens, HEAD_DIM), BF16),
            pltpu.VMEM((HEAD_DIM, kv_tokens), BF16),
            pltpu.VMEM((2, 2 * rows, cols_half), F32),
            pltpu.VMEM((SLOTS, rows, bw), F32),
            pltpu.VMEM((2, rows, bw), BF16),
            pltpu.VMEM((SENDS, rows, bw), BF16),
            pltpu.VMEM((8, stack), F32),
            pltpu.VMEM((8, stack), F32),
            pltpu.VMEM((HEAD_DIM, stack), F32),
            pltpu.VMEM((keys_step, stack), F32),
            pltpu.VMEM((keys_step, stack), F32),
            pltpu.VMEM((8, stack), F32),
            quad, dma((DOWN_SLOTS,)), two, two, dma((4,)), dma((units,)), dma((units,)), dma, dma, peer, peer,
            dma((nbg,)), dma((2, nbg)), dma, two, quad, quad,
            sends, dma((SLOTS,)), sends, sends, sends,
            dma((2, pieces // 2)), dma((2, pieces // 2)),
            pltpu.SemaphoreType.REGULAR,
        ],
        compiler_params=pltpu.CompilerParams(
            collective_id=0, has_side_effects=True, vmem_limit_bytes=67043328),
        cost_estimate=pl.CostEstimate(flops=macs, bytes_accessed=6 * ff_half * model * units, transcendentals=0),
        name="layer",
    )(u_own, x_own, x_par, gain, q_mine, q_other, kv, vt, w_gate, w_up, w_down, w_o)
    return y_out, cache


def solution(mesh):
    row_spec = P(("rep", "sp"), None)
    cache_spec = P("rep", ("tp", "sp"), None)
    other_core = [(0, 1), (1, 0), (2, 3), (3, 2)]

    def layer_block(x_in, positions, norm_gain, w_q, w_k, w_v, w_o, w_gate, w_up, w_down):
        core = (lax.axis_index("sp") % 2).astype(jnp.int32).reshape(1)
        x_par = lax.ppermute(x_in, "sp", other_core)
        cos_tab, sin_tab = rope_tables(positions)
        gain = norm_gain.reshape(1, -1)
        normed, kv, vt, q_other, q_mine = project(core, x_in, gain, cos_tab, sin_tab, w_k, w_v, w_q)
        y_out, cache = layer(normed, x_in, x_par, gain, q_mine, q_other, kv, vt, w_gate, w_up, w_down, w_o)
        return y_out, cache[:, None, :HEAD_DIM], cache[:, None, HEAD_DIM:]

    return jax.shard_map(
        layer_block,
        mesh=mesh,
        in_specs=(row_spec, P(("rep", "sp")), P(None), P(None, "tp"), P(None, "tp"), P(None, "tp"), P("tp", None), P(None, "tp"), P(None, "tp"), P("tp", None)),
        out_specs=(row_spec, cache_spec, cache_spec),
        check_vma=False,
    )
```

time: 582 us -> 507 us (0.87)
  Pallas kernels: 565 us -> 489 us
    pallas_call x1, Pallas kernels: 524 us -> 457 us  [layer(): pl.pallas_call(functools.partial(layer_kernel, rows, att, keys_step), out...]
    pallas_call x1, Pallas kernels: 40.4 us -> 32.8 us  [project(): pl.pallas_call(qkv_kernel, grid_spec=pltpu.PrefetchScalarGridSpec(num_sca...]
  transfers between devices with their start and end apart: 1 -> 1, of which waited for: 0 -> 0; matrix products, arithmetic and copies ran while one was open for 1% -> 1% of each run, Pallas kernels for 7% -> 6%
where the time goes in v3:
time: 507 us; the launch traced here: 506 us
  Pallas kernels  489 us (96%)
  local copies, waits for them, and re-layouts  11.8 us (2%)
    pallas_call x1, Pallas kernels, layer(): pl.pallas_call(functools.partial(layer_kernel, rows, att, keys_step), out...  457 us
    pallas_call x1, Pallas kernels, project(): pl.pallas_call(qkv_kernel, grid_spec=pltpu.PrefetchScalarGridSpec(num_sca...  32.8 us
  transfers between devices with their start and end apart: 1, of which 0 were waited for; matrix products, arithmetic and copies ran while one was open for 1% of the time, Pallas kernels for 6%

profile of v3, /device:TPU:5, one launch (start us, length us, event | category | flops | bytes accessed | tf_op | source)
XLA Modules:
  0.0 506.4 jit_solution(2577267712261119502)
XLA Ops:
  0.6 0.7 collective-permute-start
  1.4 0.7 convert_element_type.3
  2.1 0.1 compare_select_fusion
  2.1 3.1 fusion
  5.2 32.8 %project.1 = (bf16[1024,5120]{1,0:T(8,128)(2,1)}, bf16[2,1024,256]{2,1,0:T(8,128)(2,1)}, bf16[2,128,1024]{2,1,0:T(8,128)(2,1)}, bf16[1024,512]{1,0:T(8,128)(2,1)}, bf16[1024,512]{1,0:T(8,128)(2,1)}) custom-call(s32[1]{0:T(128)} %bitcast.core_ref, bf16[1024,5120]{1,0:T(8,128)(2,1)} %x_own.1, f32[1,5120]{1,0:T(1,128)} %bitcast.6, ...), custom_call_target="tpu_custom_call" | custom-call | flops 16106127360 | bytes 31457280 | tf_op jit(solution)/shard_map/project/pallas_call | solution.py:133
  38.0 0.0 collective-permute-done.x_par
  38.0 456.7 %layer.1 = (bf16[1024,5120]{1,0:T(8,128)(2,1)}, bf16[4096,256]{1,0:T(8,128)(2,1)}, bf16[1024,5120]{1,0:T(8,128)(2,1)}) custom-call(bf16[1024,5120]{1,0:T(8,128)(2,1)} %get-tuple-element.10.u_own, bf16[1024,5120]{1,0:T(8,128)(2,1)} %x_own.1, bf16[1024,5120]{1,0:T(8,128)(2,1)} %collective-permute-done.x_par, f32[1,5120]{1,0:T(1,128)} %bitcast.7, ...), custom_call_target="tpu_custom_call" | custom-call | flops 134217728000 | bytes 503316480 | tf_op jit(solution)/shard_map/layer/pallas_call | solution.py:776
  494.6 3.0 slice_bitcast_fusion
  497.6 8.8 %copy.14 = bf16[1024,5120]{1,0:T(8,128)(2,1)} copy(bf16[1024,5120]{1,0:T(8,128)(2,1)} %get-tuple-element.26) | data formatting | bytes 20971520
  (1 shorter events, 0.0 us)
Async XLA Ops:
  0.6 37.3 %collective-permute-start = (bf16[1024,5120]{1,0:T(8,128)(2,1)}, bf16[1024,5120]{1,0:T(8,128)(2,1)}, u32[]{:S(2)}, u32[]{:S(2)}) collective-permute-start(bf16[1024,5120]{1,0:T(8,128)(2,1)} %x_own.1), channel_id=1, source_target_pairs={{0,1},{1,0},{2,3},{3,2},{4,5},{5,4},{6,7},{7,6},{8,9},{9,8},{10,11... | collective-permute-start | bytes 31457288 | tf_op jit(solution)/shard_map/ppermute | solution.py:826

commit v4 on v3

--- a/solution.py
+++ b/solution.py
@@ -17,9 +17,10 @@
 
 SLOTS = 4
 SENDS = 4
-HOP = 6
+HOP = 7
 BACK_HOP = 8
 DOWN_SLOTS = 2
+VMEM_BYTES = 67043328
 RATE = 5, 13
 
 
@@ -86,7 +87,7 @@
             inv_buf[part, :] = total
             return carry
 
-        lax.fori_loop(0, rows // step, squares, 0, unroll=2)
+        lax.fori_loop(0, rows // step, squares, 0, unroll=4)
         mean = jnp.sum(inv_buf[...], axis=1, keepdims=True) * (1.0 / model)
         inv_buf[...] = jnp.broadcast_to(lax.rsqrt(mean + EPS), inv_buf.shape)
 
@@ -100,7 +101,7 @@
                 u_buf[pl.ds(pl.multiple_of(block * rows + i * step, step), step), cols] = u
             return carry
 
-        lax.fori_loop(0, rows // step, scale, 0, unroll=2)
+        lax.fori_loop(0, rows // step, scale, 0, unroll=4)
         k = jnp.dot(u_ref[...], wk_ref[...], preferred_element_type=F32)
         v = jnp.dot(u_ref[...], wv_ref[...], preferred_element_type=F32)
         for head in range(2):
@@ -160,7 +161,7 @@
             jax.ShapeDtypeStruct((tokens, q_cols), BF16),
             jax.ShapeDtypeStruct((tokens, q_cols), BF16),
         ],
-        compiler_params=pltpu.CompilerParams(vmem_limit_bytes=60 * 2 ** 20),
+        compiler_params=pltpu.CompilerParams(vmem_limit_bytes=VMEM_BYTES),
         cost_estimate=pl.CostEstimate(flops=2 * tokens * model * (2 * q_cols + 4 * HEAD_DIM), bytes_accessed=6 * tokens * model, transcendentals=0),
         name="project",
     )(core, x_in, gain, cos_tab, sin_tab, w_k, w_v, w_q)
@@ -259,7 +260,7 @@
                 ubuf[at, cols] = (ubuf[at, cols].astype(F32) * inv * gain_ref[:, cols]).astype(BF16)
             return carry
 
-        lax.fori_loop(0, rows // step, body, 0, unroll=2 if rows % (2 * step) == 0 else 1)
+        lax.fori_loop(0, rows // step, body, 0, unroll=4 if rows % (4 * step) == 0 else 1)
 
     all_tokens = pl.ds(0, tokens)
 
@@ -809,11 +810,63 @@
             pltpu.SemaphoreType.REGULAR,
         ],
         compiler_params=pltpu.CompilerParams(
-            collective_id=0, has_side_effects=True, vmem_limit_bytes=67043328),
+            collective_id=0, has_side_effects=True, vmem_limit_bytes=VMEM_BYTES),
         cost_estimate=pl.CostEstimate(flops=macs, bytes_accessed=6 * ff_half * model * units, transcendentals=0),
         name="layer",
     )(u_own, x_own, x_par, gain, q_mine, q_other, kv, vt, w_gate, w_up, w_down, w_o)
     return y_out, cache
+
+
+def finish_kernel(y_in, cache_in, y_out, k_out, v_out, y_buf, cache_buf, in_sem, out_sem):
+    parts = in_sem.shape[0] // 2
+    y_rows, cache_rows = y_in.shape[0] // parts, cache_in.shape[0] // parts
+    keys, values = pl.ds(0, HEAD_DIM), pl.ds(HEAD_DIM, HEAD_DIM)
+
+    def copies(i):
+        rows = pl.ds(i * y_rows, y_rows)
+        lines = pl.ds(i * cache_rows, cache_rows)
+        y_sem, c_sem = in_sem.at[i], in_sem.at[parts + i]
+        return (
+            (pltpu.make_async_copy(y_in.at[rows], y_buf.at[rows], y_sem), pltpu.make_async_copy(cache_in.at[lines], cache_buf.at[lines], c_sem)),
+            (
+                pltpu.make_async_copy(y_buf.at[rows], y_out.at[rows], out_sem.at[i]),
+                pltpu.make_async_copy(cache_buf.at[lines, keys], k_out.at[lines], out_sem.at[parts + i]),
+                pltpu.make_async_copy(cache_buf.at[lines, values], v_out.at[lines], out_sem.at[parts + parts + i]),
+            ),
+        )
+
+    every = [copies(i) for i in range(parts)]
+    for ins, _ in every:
+        for copy in ins:
+            copy.start()
+    for ins, outs in every:
+        for copy in ins:
+            copy.wait()
+        for copy in outs:
+            copy.start()
+    for _, outs in every:
+        for copy in outs:
+            copy.wait()
+
+
+def finish(y, cache):
+    parts = 8
+    head = jax.ShapeDtypeStruct((cache.shape[0], HEAD_DIM), BF16)
+    any_spec = pl.BlockSpec(memory_space=pl.ANY)
+    return pl.pallas_call(
+        finish_kernel,
+        out_shape=[jax.ShapeDtypeStruct(y.shape, BF16), head, head],
+        in_specs=[any_spec] * 2,
+        out_specs=[any_spec] * 3,
+        scratch_shapes=[
+            pltpu.VMEM(y.shape, BF16),
+            pltpu.VMEM(cache.shape, BF16),
+            pltpu.SemaphoreType.DMA((2 * parts,)),
+            pltpu.SemaphoreType.DMA((3 * parts,)),
+        ],
+        compiler_params=pltpu.CompilerParams(vmem_limit_bytes=VMEM_BYTES),
+        name="finish",
+    )(y, cache)
 
 
 def solution(mesh):
@@ -828,7 +881,8 @@
         gain = norm_gain.reshape(1, -1)
         normed, kv, vt, q_other, q_mine = project(core, x_in, gain, cos_tab, sin_tab, w_k, w_v, w_q)
         y_out, cache = layer(normed, x_in, x_par, gain, q_mine, q_other, kv, vt, w_gate, w_up, w_down, w_o)
-        return y_out, cache[:, None, :HEAD_DIM], cache[:, None, HEAD_DIM:]
+        y_out, k_cache, v_cache = finish(y_out, cache)
+        return y_out, k_cache[:, None], v_cache[:, None]
 
     return jax.shard_map(
         layer_block,

time: 507 us -> 503 us (level)
  local copies, waits for them, and re-layouts: 11.8 us -> 0 us
  Pallas kernels: 489 us -> 498 us
    pallas_call x0 -> x1, Pallas kernels: none -> 9.51 us  [finish(): pl.pallas_call(finish_kernel, out_shape=[jax.ShapeDtypeStruct(y.shape, BF...]
    unnamed x1 -> x0, local copies, waits for them, and re-layouts: 8.78 us -> none
where the time goes in v4:
time: 503 us
  Pallas kernels  498 us (99%)
    pallas_call x1, Pallas kernels, layer(): pl.pallas_call(functools.partial(layer_kernel, rows, att, keys_step), out...  456 us
    pallas_call x1, Pallas kernels, project(): pl.pallas_call(qkv_kernel, grid_spec=pltpu.PrefetchScalarGridSpec(num_sca...  32.3 us
  transfers between devices with their start and end apart: 1, of which 0 were waited for; matrix products, arithmetic and copies ran while one was open for 1% of the time, Pallas kernels for 6%

profile of v4, /device:TPU:5, one launch (start us, length us, event | category | flops | bytes accessed | tf_op | source)
XLA Modules:
  0.0 503.1 jit_solution(8124371964270486880)
XLA Ops:
  0.6 0.7 collective-permute-start
  1.4 0.7 convert_element_type.3
  2.1 0.1 compare_select_fusion
  2.1 3.1 fusion
  5.2 32.3 %project.1 = (bf16[1024,5120]{1,0:T(8,128)(2,1)}, bf16[2,1024,256]{2,1,0:T(8,128)(2,1)}, bf16[2,128,1024]{2,1,0:T(8,128)(2,1)}, bf16[1024,512]{1,0:T(8,128)(2,1)}, bf16[1024,512]{1,0:T(8,128)(2,1)}) custom-call(s32[1]{0:T(128)} %bitcast.core_ref, bf16[1024,5120]{1,0:T(8,128)(2,1)} %x_own.1, f32[1,5120]{1,0:T(1,128)} %bitcast.6, ...), custom_call_target="tpu_custom_call" | custom-call | flops 16106127360 | bytes 31457280 | tf_op jit(solution)/shard_map/project/pallas_call | solution.py:134
  37.5 0.0 collective-permute-done.x_par
  37.5 456.1 %layer.1 = (bf16[1024,5120]{1,0:T(8,128)(2,1)}, bf16[4096,256]{1,0:T(8,128)(2,1)}, bf16[1024,5120]{1,0:T(8,128)(2,1)}) custom-call(bf16[1024,5120]{1,0:T(8,128)(2,1)} %get-tuple-element.13.u_own, bf16[1024,5120]{1,0:T(8,128)(2,1)} %x_own.1, bf16[1024,5120]{1,0:T(8,128)(2,1)} %collective-permute-done.x_par, f32[1,5120]{1,0:T(1,128)} %bitcast.7, ...), custom_call_target="tpu_custom_call" | custom-call | flops 134217728000 | bytes 503316480 | tf_op jit(solution)/shard_map/layer/pallas_call | solution.py:777
  493.6 9.5 %finish.1 = (bf16[1024,5120]{1,0:T(8,128)(2,1)}, bf16[4096,128]{1,0:T(8,128)(2,1)}, bf16[4096,128]{1,0:T(8,128)(2,1)}) custom-call(bf16[1024,5120]{1,0:T(8,128)(2,1)} %get-tuple-element.18.y_in, bf16[4096,256]{1,0:T(8,128)(2,1)} %get-tuple-element.19.cache_in), custom_call_target="tpu_custom_call" | custom-call | tf_op jit(solution)/shard_map/finish/pallas_call | solution.py:856
  (1 shorter events, 0.0 us)
Async XLA Ops:
  0.6 36.9 %collective-permute-start = (bf16[1024,5120]{1,0:T(8,128)(2,1)}, bf16[1024,5120]{1,0:T(8,128)(2,1)}, u32[]{:S(2)}, u32[]{:S(2)}) collective-permute-start(bf16[1024,5120]{1,0:T(8,128)(2,1)} %x_own.1), channel_id=1, source_target_pairs={{0,1},{1,0},{2,3},{3,2},{4,5},{5,4},{6,7},{7,6},{8,9},{9,8},{10,11... | collective-permute-start | bytes 31457288 | tf_op jit(solution)/shard_map/ppermute | solution.py:879
